TPU v7x, 256 devices: a whole 4x4x8 slice. The times are simulated.
256 devices in a mesh: batch: 128 (over z, y, x_lo, core), rep: 2 (over x_hi).
Axes of the slice: x: 4 (x_hi: 2, x_lo: 2; x = x_hi * 2 + x_lo), y: 4, z: 8, core: 2. Of those that a mesh axis runs over, the one named last changes fastest.
Arguments:
- queries: bfloat16 [16384, 512], P('batch', 'rep'), may hold values from -8 to 8
- passages: bfloat16 [16384, 512], P('batch', 'rep'), may hold values from -8 to 8
- positives: int32 [16384], replicated, may hold values from 0 to 16383, each once
Outputs:
- grad_queries: float32 [16384, 512], P('batch', 'rep')
- grad_passages: float32 [16384, 512], P('batch', 'rep')
Inputs may be any that keep to these rules, and one draw needn't show every extreme that they name: `positives`: each passage is the positive of exactly one query.
All inputs are finite; a program needn't handle non-finite values.
Results may differ from a plain program's by a relative error of at most 0.0013.
Values may be sent and summed in bfloat16 or wider, within the bound.
A program may use at most 128 MiB of HBM per device.

v0:
```python
import math

import jax
import jax.numpy as jnp
from jax import lax
from jax.sharding import Mesh
from jax.sharding import PartitionSpec as P

BATCH = ("batch_0", "batch_1", "batch_2", "batch_3")


NEGATIVE = -1e30


def sent_together(arrays, axis, dim, along):
    both = jnp.concatenate(arrays, axis=along)
    filled, at, outs = (lax.all_gather(both, axis, axis=dim, tiled=True), 0, [])
    for a in arrays:
        outs.append(lax.slice_in_dim(filled, at, at + a.shape[along], axis=along))
        at += a.shape[along]
    return tuple(outs)


def copy_for_each(x, axis):
    count = lax.axis_size(axis)
    return lax.all_to_all(jnp.broadcast_to(x[None], (count, *x.shape)), axis, 0, 0, tiled=True)


def gathered_once(x, axis):
    leaves = jax.tree.leaves(x)
    order = sorted(range(len(leaves)), key=lambda k: -leaves[k].size)
    width = (1, *leaves[order[0]].shape)[-1]
    lines = [
        jnp.pad(leaves[k].reshape(-1), (0, -leaves[k].size % width)).reshape(-1, width)
        for k in order
    ]
    both, at, found = (copy_for_each(jnp.concatenate(lines), axis), 0, {})
    for k, line in zip(order, lines):
        section = both[:, at : at + len(line)].reshape(len(both), -1)
        found[k] = section[:, : leaves[k].size].reshape(-1, *leaves[k].shape)
        at += len(line)
    numbers = iter(range(len(leaves)))
    return jax.tree.map(lambda _: found[next(numbers)], x)


def combined_pairwise(pieces, combine):
    while len(jax.tree.leaves(pieces)[0]) > 1:
        pieces = jax.vmap(combine)(
            *(jax.tree.map(lambda part: part[side::2], pieces) for side in (0, 1))
        )
    return jax.tree.map(lambda part: part[0], pieces)


def joined_all(x, axis, combine):
    pieces = gathered_once(x, axis)
    return combined_pairwise(pieces, combine)


def collected_together(x, axis):
    leaves = jax.tree.leaves(x)
    order = sorted(range(len(leaves)), key=lambda k: -leaves[k].size)
    width = (1, *leaves[order[0]].shape)[-1]
    lines = [
        jnp.pad(leaves[k].reshape(-1), (0, -leaves[k].size % width)).reshape(-1, width)
        for k in order
    ]
    both, at, found = (lax.all_gather(jnp.concatenate(lines), axis), 0, {})
    for k, line in zip(order, lines):
        section = both[:, at : at + len(line)].reshape(len(both), -1)
        found[k] = section[:, : leaves[k].size].reshape(-1, *leaves[k].shape)
        at += len(line)
    numbers = iter(range(len(leaves)))
    return jax.tree.map(lambda _: found[next(numbers)], x)


def merged_by_axis(x, axes, combine):
    for axis in axes:
        pieces = collected_together(x, axis)
        x = jax.tree.map(lambda part: part[0], pieces)
        for k in range(1, lax.axis_size(axis)):
            x = combine(x, jax.tree.map(lambda part: part[k], pieces))
    return x


def joined_along(pieces, dim):
    pieces = jnp.moveaxis(pieces, 0, dim)
    dims = pieces.shape
    return pieces.reshape(*dims[:dim], dims[dim] * dims[dim + 1], *dims[dim + 2 :])


def stacked_from(x, axes, order):
    pieces = x
    for k in order:
        pieces = lax.all_gather(pieces, axes[k])
    done = order[::-1]
    back = [done.index(k) for k in range(len(axes))]
    pieces = pieces.transpose(*back, *range(len(axes), pieces.ndim))
    return pieces.reshape(-1, *x.shape)


def whole_of(x, axes, order, dim):
    return joined_along(stacked_from(x, axes, order), dim)


def collect(x, axis, dim):
    pieces = copy_for_each(x, axis)
    return joined_along(pieces, dim)


def in_blocks(x, dim, count):
    dims = x.shape
    pieces = x.reshape(*dims[:dim], count, dims[dim] // count, *dims[dim + 1 :])
    return jnp.moveaxis(pieces, dim, 0)


def summed_on_arrival(x, axis, dim):
    count = lax.axis_size(axis)
    pieces = lax.all_to_all(in_blocks(x, dim, count), axis, 0, 0, tiled=True)
    return jnp.sum(pieces, axis=0)


def sent_together_2(arrays, axis, dim, along):
    both = jnp.concatenate(arrays, axis=along)
    filled, at, outs = (summed_on_arrival(both, axis, dim), 0, [])
    for a in arrays:
        outs.append(lax.slice_in_dim(filled, at, at + a.shape[along], axis=along))
        at += a.shape[along]
    return tuple(outs)


def sweep_blocks(update, running, members):
    piece_rows = members[0].shape[0]

    def advance(carried, block_index):
        sliced = tuple(
            (lax.dynamic_slice_in_dim(member, block_index * 512, 512, 0) for member in members)
        )
        return (update(carried, sliced, block_index * 512), None)

    running, unused = lax.scan(advance, running, jnp.arange(piece_rows // 512, dtype=jnp.int32))
    return running


def combine_pairs(former, latter):
    results = []
    for position in range(0, len(former), 2):
        highest = jnp.maximum(former[position], latter[position])
        summed = former[position + 1] * jnp.exp(former[position] - highest) + latter[
            position + 1
        ] * jnp.exp(latter[position] - highest)
        results.extend([highest, summed])
    return tuple(results)


def pair_scores(local_set, remote_set, logit_scale):
    products = lax.dot_general(
        local_set, remote_set, (((1,), (1,)), ((), ())), preferred_element_type=jnp.float32
    )
    return products * logit_scale


def weighted_sum(
    local_set, local_norm, local_keys, remote_set, remote_norm, remote_keys, logit_scale
):
    scores = pair_scores(local_set, remote_set, logit_scale)
    matches = (local_keys[:, None] == remote_keys[None, :]).astype(jnp.float32)
    weights = (
        jnp.exp(scores - local_norm[:, None])
        + jnp.exp(scores - remote_norm[None, :])
        - 2.0 * matches
    )
    return jnp.dot(weights.astype(jnp.bfloat16), remote_set, preferred_element_type=jnp.float32)


def local(queries, passages, positives):
    own_rows = queries.shape[0]
    half_rows = own_rows // 2
    model_width = queries.shape[1] * lax.axis_size("rep")
    batch_count = lax.axis_size(BATCH)
    all_rows = batch_count * own_rows
    column_count = batch_count * half_rows
    logit_scale = 1.0 / math.sqrt(model_width)
    batch_index = lax.axis_index(BATCH)
    rep_index = lax.axis_index("rep")
    block_start = batch_index * own_rows
    half_start = rep_index * half_rows
    query_full, passage_full = sent_together((queries, passages), "rep", 1, 0)
    passage_half = lax.dynamic_slice_in_dim(passage_full, half_start, half_rows, 0)

    def score_update(running, sliced, offset):
        row_high, row_total, column_high, column_total = running
        scores = pair_scores(query_full, sliced[0], logit_scale)
        new_high = jnp.maximum(row_high, jnp.max(scores, axis=1))
        row_total = row_total * jnp.exp(row_high - new_high) + jnp.sum(
            jnp.exp(scores - new_high[:, None]), axis=1
        )
        piece_high = jnp.max(scores, axis=0)
        piece_total = jnp.sum(jnp.exp(scores - piece_high[None, :]), axis=0)
        column_high = lax.dynamic_update_slice_in_dim(column_high, piece_high, offset, 0)
        column_total = lax.dynamic_update_slice_in_dim(column_total, piece_total, offset, 0)
        return (new_high, row_total, column_high, column_total)

    starting = (
        jnp.full((own_rows,), NEGATIVE, jnp.float32),
        jnp.zeros((own_rows,), jnp.float32),
        jnp.full((column_count,), NEGATIVE, jnp.float32),
        jnp.zeros((column_count,), jnp.float32),
    )
    row_high, row_total, column_high, column_total = sweep_blocks(
        score_update, starting, (lax.all_gather(passage_half, BATCH, axis=0, tiled=True),)
    )
    row_high, row_total = joined_all((row_high, row_total), "rep", combine_pairs)
    column_high, column_total = merged_by_axis((column_high, column_total), BATCH, combine_pairs)
    row_norms = whole_of(row_high + jnp.log(row_total), BATCH, (2, 0, 1, 3), 0)
    column_halves = collect(column_high + jnp.log(column_total), "rep", 0)
    column_norms = (
        column_halves.reshape(2, batch_count, half_rows).transpose(1, 0, 2).reshape(all_rows)
    )
    row_own = lax.dynamic_slice_in_dim(row_norms, block_start, own_rows, 0)
    column_own = lax.dynamic_slice_in_dim(column_norms, block_start, own_rows, 0)
    positive_own = lax.dynamic_slice_in_dim(positives, block_start, own_rows, 0)
    own_ids = block_start + jnp.arange(own_rows, dtype=jnp.int32)
    all_ids = jnp.arange(all_rows, dtype=jnp.int32)
    cleared = jnp.zeros((own_rows, model_width), jnp.float32)

    def half_order(vector):
        return lax.dynamic_slice_in_dim(
            vector.reshape(batch_count, own_rows), half_start, half_rows, 1
        ).reshape(column_count)

    column_order = half_order(column_norms)
    row_order = half_order(row_norms)
    positive_order = half_order(positives)
    passage_order = half_order(all_ids)
    query_half = lax.dynamic_slice_in_dim(query_full, half_start, half_rows, 0)

    def both_update(running, sliced, offset):
        query_sum, passage_sum = running
        passage_piece, query_piece = sliced
        piece_rows = passage_piece.shape[0]

        def window(vector):
            return lax.dynamic_slice_in_dim(vector, offset, piece_rows, 0)

        query_sum = query_sum + weighted_sum(
            query_full,
            row_own,
            positive_own,
            passage_piece,
            window(column_order),
            window(passage_order),
            logit_scale,
        )
        passage_sum = passage_sum + weighted_sum(
            passage_full,
            column_own,
            own_ids,
            query_piece,
            window(row_order),
            window(positive_order),
            logit_scale,
        )
        return (query_sum, passage_sum)

    query_sum, passage_sum = sweep_blocks(
        both_update, (cleared, cleared), sent_together((passage_half, query_half), BATCH, 0, 1)
    )
    grad_queries, grad_passages = sent_together_2(
        (query_sum * logit_scale, passage_sum * logit_scale), "rep", 1, 0
    )
    return (grad_queries, grad_passages)


def solution(mesh):
    split = Mesh(
        mesh.devices.reshape(8, 4, 2, 2, mesh.shape["rep"]),
        ("batch_0", "batch_1", "batch_2", "batch_3", "rep"),
    )
    return jax.shard_map(
        local,
        mesh=split,
        in_specs=(P(BATCH, "rep"), P(BATCH, "rep"), P()),
        out_specs=(P(BATCH, "rep"), P(BATCH, "rep")),
        check_vma=False,
    )
```

profile of v0, /device:TPU:1, one launch (start us, length us, event | category | flops | bytes accessed | tf_op | source)
XLA Modules:
  0.0 584.2 jit_solution(4580716487339270084)
XLA Ops:
  8.1 6.6 %all_gather.55 = bf16[256,512]{1,0:T(8,128)(2,1)S(1)} all-gather(bf16[256,256]{1,0:T(8,128)(2,1)S(1)} %pad_maximum_fusion.1), channel_id=1, replica_groups=mesh['batch_0'=8,'batch_1'=4,'batch_2'=2,'batch_3'=2,'rep'=2] {'rep'}, dimensions={1}, use_global_device_ids=true | all-gather | bytes 393216 | tf_op jit(solution)/shard_map/all_gather | solution.py:17
  18.9 219.8 %all-gather.18.cloned.1.call-done = bf16[8192,512]{1,0:T(8,128)(2,1)} async-done(((bf16[64,512]{1,0:T(8,128)(2,1)}), bf16[8192,512]{1,0:T(8,128)(2,1)}) %all-gather.18.cloned.1.call-update) | async-done | bytes 8388624 | tf_op jit(solution)/shard_map/all_gather | solution.py:210
  238.7 55.7 %while.30 = (s32[]{:T(128)}, f32[128]{0:T(128)S(1)}, f32[128]{0:T(128)S(1)}, f32[8192]{0:T(1024)S(1)}, f32[8192]{0:T(1024)S(1)}, /*index=5*/s32[16]{0:T(128)S(1)...) while((s32[]{:T(128)}, f32[128]{0:T(128)S(1)}, ...), condition=%wide.region_5.6_spmd.clone, body=%wide.region_0.5_spmd.clone.sunk | while | flops 67567240 | bytes 1200838 | solution.py:140
  295.0 4.0 all-to-all-start
  299.0 22.2 %all-gather.9 = f32[8,2,8192]{2,1,0:T(2,128)S(1)} all-gather(f32[1,2,8192]{2,1,0:T(2,128)S(1)} %maximum_bitcast_fusion), channel_id=5, replica_groups=mesh['batch_0'=8,'batch_1'=4,'batch_2'=2,'batch_3'=2,'rep'=2] {'batch_0'}, dimensions={0}, use_global_device_ids=true | all-gather | bytes 589824 | tf_op jit(solution)/shard_map/all_gather | solution.py:67
  322.1 9.4 %all-gather.10 = f32[4,2,8192]{2,1,0:T(2,128)S(1)} all-gather(f32[1,2,8192]{2,1,0:T(2,128)S(1)} %maximum_bitcast_fusion.1), channel_id=6, replica_groups=mesh['batch_0'=8,'batch_1'=4,'batch_2'=2,'batch_3'=2,'rep'=2] {'batch_1'}, dimensions={0}, use_global_device_ids=true | all-gather | bytes 327680 | tf_op jit(solution)/shard_map/all_gather | solution.py:67
  331.9 5.0 all-gather.11
  337.1 10.3 %all-gather.12 = f32[2,2,8192]{2,1,0:T(2,128)S(1)} all-gather(f32[1,2,8192]{2,1,0:T(2,128)S(1)} %maximum_bitcast_fusion.3), channel_id=8, replica_groups=mesh['batch_0'=8,'batch_1'=4,'batch_2'=2,'batch_3'=2,'rep'=2] {'batch_3'}, dimensions={0}, use_global_device_ids=true | all-gather | bytes 196608 | tf_op jit(solution)/shard_map/all_gather | solution.py:67
  348.2 4.8 all-to-all-start.1
  353.0 3.1 all-gather.7
  356.1 12.3 %all-gather.8 = f32[8,2,128]{2,1,0:T(2,128)S(1)} all-gather(f32[1,2,128]{2,1,0:T(2,128)S(1)} %bitcast.357), channel_id=2, replica_groups=mesh['batch_0'=8,'batch_1'=4,'batch_2'=2,'batch_3'=2,'rep'=2] {'batch_0'}, dimensions={0}, use_global_device_ids=true | all-gather | bytes 9216 | tf_op jit(solution)/shard_map/all_gather | solution.py:94
  368.4 9.0 %all-gather.1 = f32[32,2,128]{2,1,0:T(2,128)S(1)} all-gather(f32[8,2,128]{2,1,0:T(2,128)S(1)} %all-gather.8), channel_id=3, replica_groups=mesh['batch_0'=8,'batch_1'=4,'batch_2'=2,'batch_3'=2,'rep'=2] {'batch_1'}, dimensions={0}, use_global_device_ids=true | all-gather | bytes 40960 | tf_op jit(solution)/shard_map/all_gather | solution.py:94
  377.4 9.8 %all-gather.2 = f32[8,8,2,128]{3,1,2,0:T(8,128)S(1)} all-gather(f32[4,8,2,128]{3,1,2,0:T(8,128)S(1)} %copy.20), channel_id=4, replica_groups=mesh['batch_0'=8,'batch_1'=4,'batch_2'=2,'batch_3'=2,'rep'=2] {'batch_3'}, dimensions={0}, use_global_device_ids=true | all-gather | bytes 98304 | tf_op jit(solution)/shard_map/all_gather | solution.py:94
  388.4 79.3 %all-gather.16.cloned.1.call-done = bf16[8192,1024]{1,0:T(8,128)(2,1)} async-done(((bf16[64,1024]{1,0:T(8,128)(2,1)}), bf16[8192,1024]{1,0:T(8,128)(2,1)}) %all-gather.16.cloned.1.call-update) | async-done | bytes 16777232 | tf_op jit(solution)/shard_map/all_gather | solution.py:17
  467.7 11.3 %fusion.101 = (bf16[8192,512]{1,0:T(8,128)(2,1)}, bf16[8192,512]{1,0:T(8,128)(2,1)}) fusion(bf16[8192,1024]{1,0:T(8,128)(2,1)} %all-gather.16.cloned.1.call-done), kind=kLoop, calls=%fused_computation.152 | loop fusion | bytes 33554432 | tf_op jit(solution)/shard_map/slice | solution.py:19
  479.0 86.1 %while.31 = (s32[]{:T(128)}, f32[128,512]{1,0:T(8,128)S(1)}, f32[128,512]{1,0:T(8,128)S(1)}, s32[16]{0:T(128)S(1)}, bf16[8192,512]{1,0:T(8,128)(2,1)}, /*index=5...) while((s32[]{:T(128)}, f32[128,512]{1,0:T(8,128)S(1)}, ...), condition=%wide.region_7.8_spmd.clone, body=%wide.region_6.7_spmd.clone.sunk | while | flops 269746304 | bytes 3438348 | solution.py:140
  480.4 2.0 convolution_add_fusion.5
  487.9 1.9 convolution_add_fusion.4
  504.0 1.9 convolution_add_fusion.4
  507.4 1.9 convolution_add_fusion.5
  528.8 1.9 convolution_add_fusion.5
  539.6 1.9 convolution_add_fusion.5
  563.1 1.9 convolution_add_fusion.4
  565.7 11.0 %all_to_all.16 = f32[2,256,256]{2,1,0:T(8,128)S(1)} all-to-all(f32[2,256,256]{2,1,0:T(8,128)S(1)} %copy.28), channel_id=1, replica_groups=mesh['batch_0'=8,'batch_1'=4,'batch_2'=2,'batch_3'=2,'rep'=2] {'rep'}, dimensions={0} | all-to-all | bytes 1048576 | tf_op jit(solution)/shard_map/all_to_all | solution.py:118
  (307 shorter events, 116.6 us)
Async XLA Ops:
  7.2 231.5 %all-gather.18.cloned.1.call-start = ((), (), s32[]{:S(2)}) async-start(), calls=%async_computation.4 | async-start | bytes 8454144 | tf_op jit(solution)/shard_map/all_gather | solution.py:210
  15.4 452.3 %all-gather.16.cloned.1.call-start = ((), (), s32[]{:S(2)}) async-start(), calls=%async_computation.3 | async-start | bytes 16908288 | tf_op jit(solution)/shard_map/all_gather | solution.py:17
  295.0 52.5 %all-to-all-start = ((f32[2,2,128]{2,1,0:T(2,128)}), f32[2,2,128]{2,1,0:T(2,128)S(1)}, u32[]{:S(2)}, u32[]{:S(2)}) async-start(f32[2,2,128]{2,1,0:T(2,128)} %broadcast_in_dim.21), calls=%async_computation | async-start | bytes 4096 | tf_op jit(solution)/shard_map/all_to_all | solution.py:26
  348.2 39.3 %all-to-all-start.1 = ((f32[2,1,8192]{2,1,0:T(1,128)}), f32[2,1,8192]{2,1,0:T(1,128)S(1)}, u32[]{:S(2)}, u32[]{:S(2)}) async-start(f32[2,1,8192]{2,1,0:T(1,128)} %broadcast_in_dim.22), calls=%async_computation.1 | async-start | bytes 131072 | tf_op jit(solution)/shard_map/all_to_all | solution.py:26
Sparse Core Ops, SparseCore 0:
  15.5 223.1 all-gather.17
  241.1 226.5 all-gather.15
where the time goes:
time: 588 us; the launch traced here: 584 us
  waiting for transfers between devices  299 us (51%)
  blocking collectives  98.6 us (17%)
  matrix products  83.6 us (14%)
  local copies, waits for them, and re-layouts  48.4 us (8%)
  loops' own time  22 us (4%)
  between operations  14.3 us (2%)
  other arithmetic  9.37 us (2%)
  starting transfers between devices  8.84 us (2%)
    all_gather x1, waiting for transfers between devices, local(): lax.all_gather(passage_half, BATCH, axis=0, tiled=True)  220 us
    all_gather x1, waiting for transfers between devices, sent_together(): filled, at, outs = (lax.all_gather(both, axis, axis=dim, tiled=True), 0, [])  79.3 us
    dot_general x32, matrix products, weighted_sum(): jnp.dot(weights.astype(jnp.bfloat16), remote_set, preferred_element_type=...  60.7 us
    all_gather x4, blocking collectives, collected_together(): both, at, found = (lax.all_gather(jnp.concatenate(lines), axis), 0, {})  46.9 us
    all_gather x4, blocking collectives, stacked_from(): pieces = lax.all_gather(pieces, axes[k])  34.1 us
    dot_general x16, matrix products, pair_scores(): lax.dot_general(local_set, remote_set, (((1,), (1,)), ((), ())), preferre...  22.9 us
    another operation x2, loops' own time, sweep_blocks(): lax.scan(advance, running, jnp.arange(piece_rows // 512, dtype=jnp.int32))  22 us
    dynamic_slice x32, local copies, waits for them, and re-layouts, sweep_blocks(): lax.scan(advance, running, jnp.arange(piece_rows // 512, dtype=jnp.int32))  18.8 us
  transfers between devices with their start and end apart: 4, of which 2 were waited for; matrix products, arithmetic and copies ran while one was open for 9% of the time, Pallas kernels for 0%

commit v1 on v0

v1 whole, which is shorter than its diff:
```python
import math

import jax
import jax.numpy as jnp
from jax import lax
from jax.experimental import pallas as pl
from jax.experimental.pallas import tpu as pltpu
from jax.sharding import Mesh
from jax.sharding import PartitionSpec as P

AXES = ("z", "y", "xl", "c", "xh")
BATCH = ("z", "y", "xl", "c")
NX, NY, NZ = 4, 4, 8
MESH = pl.DeviceIdType.MESH
ROWS = 128
HALF = 64
WIDE = 256
TILE = 1024
STEP = 32000.0
LOG2E = 1.4426950408889634
LN2 = 0.6931471805599453


def encode(x):
    top = jnp.max(jnp.abs(x), axis=0, keepdims=True)
    power = jnp.clip(jnp.floor(jnp.log(top) * LOG2E) + 1.0, -120.0, 120.0)
    value = jnp.round(x * (STEP * jnp.exp2(-power)))
    power = jnp.broadcast_to(power, (16, x.shape[1]))
    return (
        value.astype(jnp.int32).astype(jnp.int16),
        power.astype(jnp.int32).astype(jnp.int16),
    )


def decode(value, power):
    unit = jnp.exp2(power.astype(jnp.int32).astype(jnp.float32)[:1]) * (1.0 / STEP)
    return value.astype(jnp.int32).astype(jnp.float32) * unit


def to_lanes(column):
    return jnp.broadcast_to(column, (128, 128)).T[:1]


def to_rows(line):
    return jnp.broadcast_to(line, (128, 128)).T


def join(stack):
    high = jnp.max(stack, axis=0)
    return high + jnp.log(jnp.sum(jnp.exp2(stack - high[None]), axis=0)) * LOG2E


def nt(a, b):
    return lax.dot_general(a, b, (((1,), (1,)), ((), ())), preferred_element_type=jnp.float32)


def tn(a, b):
    return lax.dot_general(a, b, (((0,), (0,)), ((), ())), preferred_element_type=jnp.float32)


def kernel(
    q_ref, p_ref, pos_ref, gq_ref, gp_ref,
    Q, PT, S, W, posc, tmp, cmax, csum, rstat, cstat, rown, cown, rfin,
    XQ, GQ, SQ, RQ, SP, RP,
    s_xq, r_xq, s_p, r_p, s_q, r_q, s_d, r_d, s_rs, r_rs, s_cs, r_cs,
    s_x, r_x, s_gp, r_gp, s_gq, r_gq,
):
    z, y, xl, c, xh = (lax.axis_index(a) for a in AXES)
    x = xh * 2 + xl
    factor = 1.0 / math.sqrt(2 * WIDE)

    def copy(src, dst, ssem, rsem, **where):
        return pltpu.make_async_remote_copy(
            src_ref=src, dst_ref=dst, send_sem=ssem, recv_sem=rsem,
            device_id=where, device_id_type=MESH,
        )

    def plane(k):
        tx, ty = lax.rem(x + k % 4, NX), lax.rem(y + k // 4, NY)
        return tx, ty, {"xh": tx // 2, "xl": lax.rem(tx, 2), "y": ty}

    def plane_from(k):
        fx, fy = lax.rem(x + (4 - k % 4) % 4, NX), lax.rem(y + (4 - k // 4) % 4, NY)
        return fx, fy

    def pillar(k):
        tz, tc = lax.rem(z + k // 2, NZ), lax.rem(c + k % 2, 2)
        return tz, tc, {"z": tz, "c": tc}

    def pillar_from(k):
        return lax.rem(z + (8 - k // 2) % 8, NZ), lax.rem(c + k % 2, 2)

    barrier = pltpu.get_barrier_semaphore()
    count = 0
    for k in range(1, 16):
        for where in (plane(k)[2], pillar(k)[2]):
            pl.semaphore_signal(barrier, inc=1, device_id=where, device_id_type=MESH)
            count += 1
    for k in range(NZ):
        where = {"xh": 1 - xh, "z": lax.rem(z + k, NZ)}
        if k:
            pl.semaphore_signal(barrier, inc=1, device_id=where, device_id_type=MESH)
            count += 1
    pl.semaphore_wait(barrier, count)

    slot_q = z * 2 + c
    slot_p = y * 2 + xl
    own_rows = pl.ds(pl.multiple_of(xh * HALF, HALF), HALF)
    other_rows = pl.ds(pl.multiple_of((1 - xh) * HALF, HALF), HALF)

    sends = []
    cp = copy(q_ref.at[other_rows], Q.at[xh, slot_q], s_xq, r_xq, xh=1 - xh)
    cp.start()
    sends.append(cp)
    for k in range(1, 8):
        for_a = copy(q_ref.at[own_rows], Q.at[xh, slot_q], s_q.at[0, k], r_q.at[0, k], z=lax.rem(z + k, NZ))
        for_a.start()
        sends.append(for_a)
    for k in range(1, 16):
        cp = copy(p_ref, PT.at[xh, slot_p], s_p.at[k], r_p.at[k], **plane(k)[2])
        cp.start()
        sends.append(cp)
    copy(q_ref.at[own_rows], Q.at[1 - xh, slot_q], s_xq, r_xq, xh=1 - xh).wait_recv()
    for k in range(1, 8):
        cp = copy(Q.at[1 - xh, slot_q], Q.at[1 - xh, slot_q], s_q.at[1, k], r_q.at[1, k], z=lax.rem(z + k, NZ))
        cp.start()
        sends.append(cp)
    Q[xh, slot_q] = q_ref[own_rows, :]
    PT[xh, slot_p] = p_ref[...]
    cp = copy(q_ref.at[own_rows], Q.at[xh, slot_q], s_d.at[0], r_d.at[0], c=1 - c)
    cp.start()
    sends.append(cp)
    cp = copy(Q.at[1 - xh, slot_q], Q.at[1 - xh, slot_q], s_d.at[8], r_d.at[8], c=1 - c)
    cp.start()
    sends.append(cp)

    for s in range(16):
        line = (s // 2) * 16 + y * 4 + xl * 2 + s % 2
        tmp[...] = to_rows(pos_ref[pl.ds(line, 1), :])
        posc[s * HALF : (s + 1) * HALF] = tmp[own_rows, :]

    for k in range(1, 8):
        fz = lax.rem(z + 8 - k, NZ)
        for h, part in ((0, xh), (1, 1 - xh)):
            copy(Q.at[part, slot_q], Q.at[part, fz * 2 + c], s_q.at[h, k], r_q.at[h, k], z=fz).wait_recv()
        cp = copy(Q.at[:, fz * 2 + c], Q.at[:, fz * 2 + c], s_d.at[k], r_d.at[k], c=1 - c)
        cp.start()
        sends.append(cp)
    for k in range(1, 16):
        fx, fy = plane_from(k)
        copy(p_ref, PT.at[fx // 2, fy * 2 + lax.rem(fx, 2)], s_p.at[k], r_p.at[k], c=1 - c).wait_recv()
    for k in range(0, 8):
        fz = lax.rem(z + 8 - k, NZ)
        if k == 0:
            copy(q_ref.at[own_rows], Q.at[xh, z * 2 + 1 - c], s_d.at[0], r_d.at[0], c=1 - c).wait_recv()
            copy(q_ref.at[own_rows], Q.at[1 - xh, z * 2 + 1 - c], s_d.at[8], r_d.at[8], c=1 - c).wait_recv()
        else:
            copy(Q.at[:, slot_q], Q.at[:, fz * 2 + 1 - c], s_d.at[k], r_d.at[k], c=1 - c).wait_recv()

    def score(i, carry):
        rows = pl.ds(pl.multiple_of(i * 128, 128), 128)
        part = [
            nt(Q[h, pl.ds(i * 2, 2)].reshape(128, WIDE), PT[h].reshape(TILE, WIDE))
            for h in range(2)
        ]
        s = (part[0] + part[1]) * (factor * LOG2E)
        S[rows] = s
        high = jnp.max(s, axis=1, keepdims=True)
        total = jnp.sum(jnp.exp2(s - high), axis=1, keepdims=True)
        rown[pl.ds(i, 1)] = to_lanes(high + jnp.log(total) * LOG2E)
        chigh = jnp.max(s, axis=0, keepdims=True)
        cmax[pl.ds(i, 1)] = chigh
        csum[pl.ds(i, 1)] = jnp.sum(jnp.exp2(s - chigh), axis=0, keepdims=True)
        return carry

    lax.fori_loop(0, 8, score, 0)
    chigh = jnp.max(cmax[...], axis=0, keepdims=True)
    ctotal = jnp.sum(csum[...] * jnp.exp2(cmax[...] - chigh), axis=0, keepdims=True)
    cnorm = chigh + jnp.log(ctotal) * LOG2E
    for b in range(8):
        cown[b : b + 1] = cnorm[:, b * 128 : (b + 1) * 128]
    rstat[0] = rown[...]
    cstat[0] = cown[...]
    for k in range(1, 16):
        cp = copy(rown, rstat.at[k], s_rs.at[k], r_rs.at[k], **pillar(k)[2])
        cp.start()
        sends.append(cp)
        cp = copy(cown, cstat.at[k], s_cs.at[k], r_cs.at[k], **plane(k)[2])
        cp.start()
        sends.append(cp)
    for k in range(1, 16):
        copy(rown, rstat.at[k], s_rs.at[k], r_rs.at[k], **pillar(k)[2]).wait_recv()
        copy(cown, cstat.at[k], s_cs.at[k], r_cs.at[k], **plane(k)[2]).wait_recv()
    rown2 = join(rstat[...])
    cown2 = join(cstat[...])
    cmax[0:1] = jnp.concatenate([cown2[b : b + 1] for b in range(8)], axis=1)
    rfin[...] = rown2

    def weigh(i, carry):
        rows = pl.ds(pl.multiple_of(i * 128, 128), 128)
        rnorm = to_rows(rfin[pl.ds(i, 1), :])
        for b in range(8):
            cols = slice(b * 128, (b + 1) * 128)
            s = S[rows, cols]
            first = ((z * 4 + b // 2) * 2 + b % 2) * 2 + c
            ids = first * ROWS + lax.broadcasted_iota(jnp.int32, (128, 128), 1)
            match = jnp.where(posc[rows, :] == ids, 2.0, 0.0)
            w = jnp.exp2(s - rnorm) + jnp.exp2(s - cmax[0:1, cols]) - match
            W[rows, cols] = w.astype(jnp.bfloat16)
        return carry

    lax.fori_loop(0, 8, weigh, 0)

    for k in range(8):
        tz = lax.rem(z + k, NZ)
        rows = pl.ds(pl.multiple_of(tz * 128, 128), 128)
        for h in range(2):
            part = jnp.dot(W[rows, :], PT[h].reshape(TILE, WIDE), preferred_element_type=jnp.float32)
            tmp2 = part.reshape(2, HALF, WIDE)
            GQ[k, 0, h] = tmp2[0]
            GQ[k, 1, h] = tmp2[1]
        cp = copy(GQ.at[k, 1 - c], XQ.at[k], s_x.at[k], r_x.at[k], c=1 - c)
        cp.start()
        sends.append(cp)

    def send_queries(k):
        copy(GQ.at[k, 1 - c], XQ.at[k], s_x.at[k], r_x.at[k], c=1 - c).wait_recv()
        tz = lax.rem(z + k, NZ)
        for d in range(2):
            h = lax.rem(xh + d, 2)
            value, power = encode(GQ[k, c, h] + XQ[k, h])
            if k == 0 and d == 0:
                RQ[0, 0, 0:HALF] = value
                RQ[0, 0, HALF:] = power
                continue
            SQ[k, d, 0:HALF] = value
            SQ[k, d, HALF:] = power
            cp = copy(SQ.at[k, d], RQ.at[k, d], s_gq.at[k, d], r_gq.at[k, d], z=tz, xh=h)
            cp.start()
            sends.append(cp)

    order = [k for k in range(1, 16)] + [0]
    for n, k in enumerate(order):
        tx, ty, where = plane(k)
        cols = pl.ds(pl.multiple_of((ty * 2 + lax.rem(tx, 2)) * 128, 128), 128)
        value, power = encode(tn(W[:, cols], Q[tx // 2].reshape(TILE, WIDE)))
        if k == 0:
            RP[0, 0:ROWS] = value
            RP[0, ROWS:] = power
        else:
            SP[k, 0:ROWS] = value
            SP[k, ROWS:] = power
            cp = copy(SP.at[k], RP.at[k], s_gp.at[k], r_gp.at[k], **where)
            cp.start()
            sends.append(cp)
        if n % 2 == 1:
            send_queries((n // 2 + 1) % 8)

    total = jnp.zeros((ROWS, WIDE), jnp.float32)
    for k in range(16):
        if k:
            copy(SP.at[k], RP.at[k], s_gp.at[k], r_gp.at[k], **plane(k)[2]).wait_recv()
        total = total + decode(RP[k, 0:ROWS], RP[k, ROWS:])
    gp_ref[...] = total * factor
    for d in range(2):
        total = jnp.zeros((HALF, WIDE), jnp.float32)
        for k in range(8):
            if k or d:
                copy(SQ.at[k, d], RQ.at[k, d], s_gq.at[k, d], r_gq.at[k, d], z=lax.rem(z + k, NZ)).wait_recv()
            total = total + decode(RQ[k, d, 0:HALF], RQ[k, d, HALF:])
        gq_ref[(own_rows, other_rows)[d], :] = total * factor
    for cp in sends:
        cp.wait_send()


def local(queries, passages, positives):
    dma = pltpu.SemaphoreType.DMA
    vmem = pl.BlockSpec(memory_space=pltpu.VMEM)
    out = jax.ShapeDtypeStruct((ROWS, WIDE), jnp.float32)
    bf16, f32, i16 = jnp.bfloat16, jnp.float32, jnp.int16
    return pl.pallas_call(
        kernel,
        out_shape=(out, out),
        in_specs=[vmem] * 3,
        out_specs=(vmem, vmem),
        scratch_shapes=[
            pltpu.VMEM((2, 16, HALF, WIDE), bf16),
            pltpu.VMEM((2, 8, ROWS, WIDE), bf16),
            pltpu.VMEM((TILE, TILE), f32),
            pltpu.VMEM((TILE, TILE), bf16),
            pltpu.VMEM((TILE, 128), jnp.int32),
            pltpu.VMEM((128, 128), jnp.int32),
            pltpu.VMEM((8, TILE), f32),
            pltpu.VMEM((8, TILE), f32),
            pltpu.VMEM((16, 8, 128), f32),
            pltpu.VMEM((16, 8, 128), f32),
            pltpu.VMEM((8, 128), f32),
            pltpu.VMEM((8, 128), f32),
            pltpu.VMEM((8, 128), f32),
            pltpu.VMEM((8, 2, HALF, WIDE), f32),
            pltpu.VMEM((8, 2, 2, HALF, WIDE), f32),
            pltpu.VMEM((8, 2, HALF + 16, WIDE), i16),
            pltpu.VMEM((8, 2, HALF + 16, WIDE), i16),
            pltpu.VMEM((16, ROWS + 16, WIDE), i16),
            pltpu.VMEM((16, ROWS + 16, WIDE), i16),
            dma, dma,
            dma((16,)), dma((16,)),
            dma((2, 8)), dma((2, 8)),
            dma((9,)), dma((9,)),
            dma((16,)), dma((16,)),
            dma((16,)), dma((16,)),
            dma((8,)), dma((8,)),
            dma((16,)), dma((16,)),
            dma((8, 2)), dma((8, 2)),
        ],
        compiler_params=pltpu.CompilerParams(
            collective_id=0, has_side_effects=True, vmem_limit_bytes=60 * 1024 * 1024
        ),
    )(queries, passages, positives.reshape(128, 128))


def solution(mesh):
    split = Mesh(
        mesh.devices.reshape(NZ, NY, 2, 2, mesh.shape["rep"]),
        AXES,
    )
    return jax.shard_map(
        local,
        mesh=split,
        in_specs=(P(BATCH, "xh"), P(BATCH, "xh"), P()),
        out_specs=(P(BATCH, "xh"), P(BATCH, "xh")),
        check_vma=False,
    )
```

time: 588 us -> 71.2 us (0.12)
  waiting for transfers between devices: 299 us -> 0 us
  blocking collectives: 98.6 us -> 0 us
  matrix products: 83.6 us -> 0 us
  Pallas kernels: 0 us -> 67.7 us
  local copies, waits for them, and re-layouts: 48.4 us -> 2.26 us
  loops' own time: 22 us -> 0 us
  between operations: 14.3 us -> 0.65 us
  other arithmetic: 9.37 us -> 0 us
  starting transfers between devices: 8.84 us -> 0 us
    all_gather x2 -> x0, waiting for transfers between devices: 299 us -> none  [the longest x1 220 us: local(): lax.all_gather(passage_half, BATCH, axis=0, tiled=True)]
    all_gather x9 -> x0, blocking collectives: 87.6 us -> none  [the longest x4 46.9 us: collected_together(): both, at, found = (lax.all_gather(jnp.concatenate(lines), axis), 0, {})]
    dot_general x48 -> x0, matrix products: 83.6 us -> none  [the longest x32 60.7 us: weighted_sum(): jnp.dot(weights.astype(jnp.bfloat16), remote_set, preferred_element_type=...]
    pallas_call x0 -> x1, Pallas kernels: none -> 67.7 us  [local(): pl.pallas_call(kernel, out_shape=(out, out), in_specs=[vmem] * 3, out_spe...]
    dynamic_slice x104 -> x0, local copies, waits for them, and re-layouts: 25.4 us -> none  [the longest x32 18.8 us: sweep_blocks(): lax.scan(advance, running, jnp.arange(piece_rows // 512, dtype=jnp.int32))]
    another operation x2 -> x0, loops' own time: 22 us -> none  [sweep_blocks(): lax.scan(advance, running, jnp.arange(piece_rows // 512, dtype=jnp.int32))]
    slice x4 -> x0, local copies, waits for them, and re-layouts: 12.1 us -> none  [the longest x2 11.3 us: sent_together(): outs.append(lax.slice_in_dim(filled, at, at + a.shape[along], axis=along))]
    all_to_all x1 -> x0, blocking collectives: 11 us -> none  [summed_on_arrival(): pieces = lax.all_to_all(in_blocks(x, dim, count), axis, 0, 0, tiled=True)]
  transfers between devices with their start and end apart: 4 -> 0, of which waited for: 2 -> 0; matrix products, arithmetic and copies ran while one was open for 9% -> 0% of each run, Pallas kernels for 0% -> 0%
where the time goes in v1:
time: 71.2 us; the launch traced here: 70.6 us
  Pallas kernels  67.7 us (95%)
  local copies, waits for them, and re-layouts  2.26 us (3%)
    pallas_call x1, Pallas kernels, local(): pl.pallas_call(kernel, out_shape=(out, out), in_specs=[vmem] * 3, out_spe...  67.7 us
    unnamed x4, local copies, waits for them, and re-layouts  2.26 us

profile of v1, /device:TPU:1, one launch (start us, length us, event | category | flops | bytes accessed | tf_op | source)
XLA Modules:
  0.0 70.6 jit_solution(11252960240194813925)
XLA Ops:
  0.6 67.7 %shard_map.50 = (f32[128,256]{1,0:T(8,128)}, f32[128,256]{1,0:T(8,128)}) custom-call(bf16[128,256]{1,0:T(8,128)(2,1)} %q_ref.1, bf16[128,256]{1,0:T(8,128)(2,1)} %p_ref.1, s32[128,128]{1,0:T(8,128)} %bitcast.1), custom_call_target="tpu_custom_call" | custom-call | tf_op jit(solution)/shard_map/pallas_call | solution.py:281
  68.3 0.0 copy-start
  68.3 1.6 %copy.7 = f32[128,256]{1,0:T(8,128)} copy(f32[128,256]{1,0:T(8,128)} %get-tuple-element.4) | data formatting | bytes 262144
  69.9 0.0 copy-done
  69.9 0.7 copy.8
Async XLA Ops:
  68.3 1.6 %copy-start = (f32[128,256]{1,0:T(8,128)S(1)}, f32[128,256]{1,0:T(8,128)}, u32[]{:S(2)}) copy-start(f32[128,256]{1,0:T(8,128)} %get-tuple-element.5) | copy-start | bytes 393220

commit v2 on v1

--- a/solution.py
+++ b/solution.py
@@ -62,7 +62,7 @@
     q_ref, p_ref, pos_ref, gq_ref, gp_ref,
     Q, PT, S, W, posc, tmp, cmax, csum, rstat, cstat, rown, cown, rfin,
     XQ, GQ, SQ, RQ, SP, RP,
-    s_xq, r_xq, s_p, r_p, s_q, r_q, s_d, r_d, s_rs, r_rs, s_cs, r_cs,
+    relay, s_xq, r_xq, s_p, r_p, s_q, r_q, s_d, r_d, s_rs, r_rs, s_cs, r_cs,
     s_x, r_x, s_gp, r_gp, s_gq, r_gq,
 ):
     z, y, xl, c, xh = (lax.axis_index(a) for a in AXES)
@@ -79,83 +79,206 @@
         tx, ty = lax.rem(x + k % 4, NX), lax.rem(y + k // 4, NY)
         return tx, ty, {"xh": tx // 2, "xl": lax.rem(tx, 2), "y": ty}
 
-    def plane_from(k):
-        fx, fy = lax.rem(x + (4 - k % 4) % 4, NX), lax.rem(y + (4 - k // 4) % 4, NY)
-        return fx, fy
-
     def pillar(k):
         tz, tc = lax.rem(z + k // 2, NZ), lax.rem(c + k % 2, 2)
         return tz, tc, {"z": tz, "c": tc}
 
-    def pillar_from(k):
-        return lax.rem(z + (8 - k // 2) % 8, NZ), lax.rem(c + k % 2, 2)
-
+    near = (
+        {"xh": lax.rem(x + 1, NX) // 2, "xl": 1 - xl},
+        {"xh": lax.rem(x + 3, NX) // 2, "xl": 1 - xl},
+        {"y": lax.rem(y + 1, NY)},
+        {"y": lax.rem(y + 3, NY)},
+        {"z": lax.rem(z + 1, NZ)},
+        {"z": lax.rem(z + 7, NZ)},
+        {"c": 1 - c},
+    )
     barrier = pltpu.get_barrier_semaphore()
-    count = 0
-    for k in range(1, 16):
-        for where in (plane(k)[2], pillar(k)[2]):
-            pl.semaphore_signal(barrier, inc=1, device_id=where, device_id_type=MESH)
-            count += 1
-    for k in range(NZ):
-        where = {"xh": 1 - xh, "z": lax.rem(z + k, NZ)}
-        if k:
-            pl.semaphore_signal(barrier, inc=1, device_id=where, device_id_type=MESH)
-            count += 1
-    pl.semaphore_wait(barrier, count)
+    for where in near:
+        pl.semaphore_signal(barrier, inc=1, device_id=where, device_id_type=MESH)
+    pl.semaphore_wait(barrier, len(near))
+    for where in near[:2]:
+        pl.semaphore_signal(relay, inc=1, device_id=where, device_id_type=MESH)
 
     slot_q = z * 2 + c
-    slot_p = y * 2 + xl
-    own_rows = pl.ds(pl.multiple_of(xh * HALF, HALF), HALF)
-    other_rows = pl.ds(pl.multiple_of((1 - xh) * HALF, HALF), HALF)
-
+    half_rows = (
+        pl.ds(pl.multiple_of(xh * HALF, HALF), HALF),
+        pl.ds(pl.multiple_of((1 - xh) * HALF, HALF), HALF),
+    )
+    own_rows, other_rows = half_rows
     sends = []
-    cp = copy(q_ref.at[other_rows], Q.at[xh, slot_q], s_xq, r_xq, xh=1 - xh)
-    cp.start()
-    sends.append(cp)
-    for k in range(1, 8):
-        for_a = copy(q_ref.at[own_rows], Q.at[xh, slot_q], s_q.at[0, k], r_q.at[0, k], z=lax.rem(z + k, NZ))
-        for_a.start()
-        sends.append(for_a)
-    for k in range(1, 16):
-        cp = copy(p_ref, PT.at[xh, slot_p], s_p.at[k], r_p.at[k], **plane(k)[2])
+
+    def start(cp):
         cp.start()
         sends.append(cp)
-    copy(q_ref.at[own_rows], Q.at[1 - xh, slot_q], s_xq, r_xq, xh=1 - xh).wait_recv()
-    for k in range(1, 8):
-        cp = copy(Q.at[1 - xh, slot_q], Q.at[1 - xh, slot_q], s_q.at[1, k], r_q.at[1, k], z=lax.rem(z + k, NZ))
-        cp.start()
-        sends.append(cp)
+
+    def ring_items():
+        a_of = lambda h, d: (h * HALF + (0 if d > 0 else 32), 32)
+        own, rounds = (0, 0), ([], [], [], [])
+        for d in (1, -1):
+            for axis in (0, 1):
+                turn = lambda o: o if axis == 0 else (o[1], o[0])
+                first, second = (0, 1) if axis == 0 else (1, 0)
+                rounds[0].append((axis, d, own, first * HALF, HALF, ()))
+        for d in (1, -1):
+            for axis in (0, 1):
+                first, second = (0, 1) if axis == 0 else (1, 0)
+                rounds[0].append((axis, d, own, second * HALF, HALF, ()))
+        for d in (1, -1):
+            for axis in (0, 1):
+                turn = lambda o: o if axis == 0 else (o[1], o[0])
+                first, second = (0, 1) if axis == 0 else (1, 0)
+                rounds[1].append((axis, d, turn((-d, 0)), *a_of(first, d)))
+        for e in (1, -1):
+            for d in (1, -1):
+                for axis in (0, 1):
+                    turn = lambda o: o if axis == 0 else (o[1], o[0])
+                    first, second = (0, 1) if axis == 0 else (1, 0)
+                    rounds[1].append((axis, d, turn((0, e)), second * HALF, HALF))
+        for d in (1, -1):
+            for axis in (0, 1):
+                turn = lambda o: o if axis == 0 else (o[1], o[0])
+                first, second = (0, 1) if axis == 0 else (1, 0)
+                rounds[1].append((axis, d, turn((-d, 0)), *a_of(second, d)))
+        for d in (1, -1):
+            for axis in (0, 1):
+                turn = lambda o: o if axis == 0 else (o[1], o[0])
+                first, second = (0, 1) if axis == 0 else (1, 0)
+                rounds[2].append((axis, d, turn((0, 2)), second * HALF, HALF))
+        for e in (1, -1):
+            for d in (1, -1):
+                for axis in (0, 1):
+                    turn = lambda o: o if axis == 0 else (o[1], o[0])
+                    first, second = (0, 1) if axis == 0 else (1, 0)
+                    rounds[2].append((axis, d, turn((-d, e)), *a_of(second, d)))
+        for d in (1, -1):
+            for axis in (0, 1):
+                turn = lambda o: o if axis == 0 else (o[1], o[0])
+                first, second = (0, 1) if axis == 0 else (1, 0)
+                rounds[3].append((axis, d, turn((-d, 2)), *a_of(second, d)))
+        return [[(*item[:2], (item[2][0] % 4, item[2][1] % 4), *item[3:5]) for item in r] for r in rounds]
+
+    rounds = ring_items()
+    numbers = {item: n for n, item in enumerate(i for r in rounds for i in r)}
+    arrived = set()
+
+    def plane_copy(item, number, sender):
+        axis, d, (dx, dy), first, rows = item
+        if not sender:
+            dx, dy = (dx - d, dy) if axis == 0 else (dx, dy - d)
+        ox, oy = lax.rem(x + dx % 4, NX), lax.rem(y + dy % 4, NY)
+        rows = pl.ds(first, rows)
+        dst = PT.at[ox // 2, oy * 2 + lax.rem(ox, 2), rows]
+        src = p_ref.at[rows] if item[2] == (0, 0) else dst
+        return copy(src, dst, s_p.at[number], r_p.at[number], **near[axis * 2 + (d < 0)])
+
+    def plane_wait(items):
+        for item in items:
+            if item not in arrived:
+                arrived.add(item)
+                plane_copy(item, numbers[item], False).wait_recv()
+
+    def needs(item):
+        axis, d, origin, first, rows = item
+        found = []
+        for other in numbers:
+            oa, od, (ox, oy), of, orows = other
+            got = ((ox - od) % 4, oy) if oa == 0 else (ox, (oy - od) % 4)
+            if got == origin and of < first + rows and first < of + orows:
+                found.append(other)
+        return found
+
+    def plane_round(n):
+        for item in rounds[n]:
+            if item[2] != (0, 0):
+                plane_wait(needs(item))
+            start(plane_copy(item, numbers[item], True))
+
+    def ring_copy(d, step, part, sender):
+        back = step - 1 if sender else step
+        oz = lax.rem(z + (NZ - back * d) % NZ, NZ)
+        rows = pl.ds((part % 2) * 32, 32)
+        h = xh if part < 2 else 1 - xh
+        dst = Q.at[h, oz * 2 + c, rows]
+        src = dst
+        if sender and step == 1 and part < 2:
+            src = q_ref.at[pl.ds(pl.multiple_of(xh * HALF + part * 32, 32), 32)]
+        number = ((d < 0) * 4 + step - 1) * 4 + part
+        return copy(src, dst, s_q.at[number], r_q.at[number], **near[4 + (d < 0)])
+
+    def carried(d, step, part):
+        return step < 4 or part % 2 == (d < 0)
+
+    def ring_send(step, group):
+        for d in (1, -1):
+            for part in (group * 2, group * 2 + 1):
+                if carried(d, step, part):
+                    start(ring_copy(d, step, part, True))
+
+    def across(k, group, source):
+        h = xh if group == 0 else 1 - xh
+        oz = lax.rem(z + k, NZ)
+        sc = c if source else 1 - c
+        dst = Q.at[h, oz * 2 + sc]
+        src = q_ref.at[own_rows] if k == 0 and group == 0 else Q.at[h, oz * 2 + c]
+        return copy(src, dst, s_d.at[k, group], r_d.at[k, group], c=1 - c)
+
+    def ring_wait(step, group):
+        for d in (1, -1):
+            for part in (group * 2, group * 2 + 1):
+                if carried(d, step, part):
+                    ring_copy(d, step, part, False).wait_recv()
+
+    def pass_across(step, group):
+        for k in {(NZ - step) % NZ, step % NZ}:
+            start(across(k, group, True))
+
+    exchange = copy(q_ref.at[other_rows], Q.at[xh, slot_q], s_xq, r_xq, xh=1 - xh)
+    plane_round(0)
+    ring_send(1, 0)
+    pl.semaphore_wait(relay, 2)
+    start(exchange)
     Q[xh, slot_q] = q_ref[own_rows, :]
-    PT[xh, slot_p] = p_ref[...]
-    cp = copy(q_ref.at[own_rows], Q.at[xh, slot_q], s_d.at[0], r_d.at[0], c=1 - c)
-    cp.start()
-    sends.append(cp)
-    cp = copy(Q.at[1 - xh, slot_q], Q.at[1 - xh, slot_q], s_d.at[8], r_d.at[8], c=1 - c)
-    cp.start()
-    sends.append(cp)
+    PT[xh, y * 2 + xl] = p_ref[...]
+    start(across(0, 0, True))
 
     for s in range(16):
         line = (s // 2) * 16 + y * 4 + xl * 2 + s % 2
         tmp[...] = to_rows(pos_ref[pl.ds(line, 1), :])
         posc[s * HALF : (s + 1) * HALF] = tmp[own_rows, :]
 
-    for k in range(1, 8):
-        fz = lax.rem(z + 8 - k, NZ)
-        for h, part in ((0, xh), (1, 1 - xh)):
-            copy(Q.at[part, slot_q], Q.at[part, fz * 2 + c], s_q.at[h, k], r_q.at[h, k], z=fz).wait_recv()
-        cp = copy(Q.at[:, fz * 2 + c], Q.at[:, fz * 2 + c], s_d.at[k], r_d.at[k], c=1 - c)
-        cp.start()
-        sends.append(cp)
-    for k in range(1, 16):
-        fx, fy = plane_from(k)
-        copy(p_ref, PT.at[fx // 2, fy * 2 + lax.rem(fx, 2)], s_p.at[k], r_p.at[k], c=1 - c).wait_recv()
-    for k in range(0, 8):
-        fz = lax.rem(z + 8 - k, NZ)
-        if k == 0:
-            copy(q_ref.at[own_rows], Q.at[xh, z * 2 + 1 - c], s_d.at[0], r_d.at[0], c=1 - c).wait_recv()
-            copy(q_ref.at[own_rows], Q.at[1 - xh, z * 2 + 1 - c], s_d.at[8], r_d.at[8], c=1 - c).wait_recv()
-        else:
-            copy(Q.at[:, slot_q], Q.at[:, fz * 2 + 1 - c], s_d.at[k], r_d.at[k], c=1 - c).wait_recv()
+    ring_wait(1, 0)
+    ring_send(2, 0)
+    plane_round(1)
+    copy(q_ref.at[own_rows], Q.at[1 - xh, slot_q], s_xq, r_xq, xh=1 - xh).wait_recv()
+    ring_send(1, 1)
+    pass_across(1, 0)
+    start(across(0, 1, True))
+    ring_wait(2, 0)
+    ring_send(3, 0)
+    plane_round(2)
+    ring_wait(1, 1)
+    ring_send(2, 1)
+    pass_across(2, 0)
+    pass_across(1, 1)
+    ring_wait(3, 0)
+    ring_send(4, 0)
+    plane_round(3)
+    ring_wait(2, 1)
+    ring_send(3, 1)
+    pass_across(3, 0)
+    pass_across(2, 1)
+    ring_wait(4, 0)
+    pass_across(4, 0)
+    ring_wait(3, 1)
+    ring_send(4, 1)
+    pass_across(3, 1)
+    for r in rounds:
+        plane_wait(r)
+    ring_wait(4, 1)
+    pass_across(4, 1)
+    for k in range(NZ):
+        for group in range(2):
+            across(k, group, False).wait_recv()
 
     def score(i, carry):
         rows = pl.ds(pl.multiple_of(i * 128, 128), 128)
@@ -303,10 +426,11 @@
             pltpu.VMEM((8, 2, HALF + 16, WIDE), i16),
             pltpu.VMEM((16, ROWS + 16, WIDE), i16),
             pltpu.VMEM((16, ROWS + 16, WIDE), i16),
+            pltpu.SemaphoreType.REGULAR,
             dma, dma,
-            dma((16,)), dma((16,)),
-            dma((2, 8)), dma((2, 8)),
-            dma((9,)), dma((9,)),
+            dma((40,)), dma((40,)),
+            dma((32,)), dma((32,)),
+            dma((8, 2)), dma((8, 2)),
             dma((16,)), dma((16,)),
             dma((16,)), dma((16,)),
             dma((8,)), dma((8,)),

time: 71.2 us -> 74.3 us (1.044)
  Pallas kernels: 67.7 us -> 71.3 us
    pallas_call x1, Pallas kernels: 67.7 us -> 71.3 us  [local(): pl.pallas_call(kernel, out_shape=(out, out), in_specs=[vmem] * 3, out_spe...]
where the time goes in v2:
time: 74.3 us; the launch traced here: 74.2 us
  Pallas kernels  71.3 us (96%)
  local copies, waits for them, and re-layouts  2.26 us (3%)
    pallas_call x1, Pallas kernels, local(): pl.pallas_call(kernel, out_shape=(out, out), in_specs=[vmem] * 3, out_spe...  71.3 us
    unnamed x4, local copies, waits for them, and re-layouts  2.26 us

profile of v2, /device:TPU:1, one launch (start us, length us, event | category | flops | bytes accessed | tf_op | source)
XLA Modules:
  0.0 74.2 jit_solution(8455231576725000503)
XLA Ops:
  0.6 71.3 %shard_map.50 = (f32[128,256]{1,0:T(8,128)}, f32[128,256]{1,0:T(8,128)}) custom-call(bf16[128,256]{1,0:T(8,128)(2,1)} %q_ref.1, bf16[128,256]{1,0:T(8,128)(2,1)} %p_ref.1, s32[128,128]{1,0:T(8,128)} %bitcast.1), custom_call_target="tpu_custom_call" | custom-call | tf_op jit(solution)/shard_map/pallas_call | solution.py:404
  71.9 0.0 copy-start
  71.9 1.6 %copy.7 = f32[128,256]{1,0:T(8,128)} copy(f32[128,256]{1,0:T(8,128)} %get-tuple-element.4) | data formatting | bytes 262144
  73.5 0.0 copy-done
  73.5 0.7 copy.8
Async XLA Ops:
  71.9 1.6 %copy-start = (f32[128,256]{1,0:T(8,128)S(1)}, f32[128,256]{1,0:T(8,128)}, u32[]{:S(2)}) copy-start(f32[128,256]{1,0:T(8,128)} %get-tuple-element.5) | copy-start | bytes 393220

commit v3 on v1

--- a/solution.py
+++ b/solution.py
@@ -79,85 +79,137 @@
         tx, ty = lax.rem(x + k % 4, NX), lax.rem(y + k // 4, NY)
         return tx, ty, {"xh": tx // 2, "xl": lax.rem(tx, 2), "y": ty}
 
-    def plane_from(k):
-        fx, fy = lax.rem(x + (4 - k % 4) % 4, NX), lax.rem(y + (4 - k // 4) % 4, NY)
-        return fx, fy
-
     def pillar(k):
         tz, tc = lax.rem(z + k // 2, NZ), lax.rem(c + k % 2, 2)
         return tz, tc, {"z": tz, "c": tc}
 
-    def pillar_from(k):
-        return lax.rem(z + (8 - k // 2) % 8, NZ), lax.rem(c + k % 2, 2)
+    def along(axis, e):
+        if axis == 0:
+            t = lax.rem(x + e, NX)
+            return {"xh": t // 2, "xl": lax.rem(t, 2)}
+        return {"y": lax.rem(y + e, NY)} if axis == 1 else {"z": lax.rem(z + e, NZ)}
 
     barrier = pltpu.get_barrier_semaphore()
-    count = 0
-    for k in range(1, 16):
-        for where in (plane(k)[2], pillar(k)[2]):
-            pl.semaphore_signal(barrier, inc=1, device_id=where, device_id_type=MESH)
-            count += 1
-    for k in range(NZ):
-        where = {"xh": 1 - xh, "z": lax.rem(z + k, NZ)}
-        if k:
-            pl.semaphore_signal(barrier, inc=1, device_id=where, device_id_type=MESH)
-            count += 1
-    pl.semaphore_wait(barrier, count)
+    near = [along(axis, e) for e in (1, 2, 3) for axis in (0, 1)]
+    near += [along(2, e) for e in (1, 7, 2, 6)] + [{"c": 1 - c}]
+    for where in near:
+        pl.semaphore_signal(barrier, inc=1, device_id=where, device_id_type=MESH)
+    pl.semaphore_wait(barrier, len(near))
 
     slot_q = z * 2 + c
     slot_p = y * 2 + xl
     own_rows = pl.ds(pl.multiple_of(xh * HALF, HALF), HALF)
     other_rows = pl.ds(pl.multiple_of((1 - xh) * HALF, HALF), HALF)
-
     sends = []
-    cp = copy(q_ref.at[other_rows], Q.at[xh, slot_q], s_xq, r_xq, xh=1 - xh)
-    cp.start()
-    sends.append(cp)
-    for k in range(1, 8):
-        for_a = copy(q_ref.at[own_rows], Q.at[xh, slot_q], s_q.at[0, k], r_q.at[0, k], z=lax.rem(z + k, NZ))
-        for_a.start()
-        sends.append(for_a)
-    for k in range(1, 16):
-        cp = copy(p_ref, PT.at[xh, slot_p], s_p.at[k], r_p.at[k], **plane(k)[2])
+
+    def start(cp):
         cp.start()
         sends.append(cp)
-    copy(q_ref.at[own_rows], Q.at[1 - xh, slot_q], s_xq, r_xq, xh=1 - xh).wait_recv()
-    for k in range(1, 8):
-        cp = copy(Q.at[1 - xh, slot_q], Q.at[1 - xh, slot_q], s_q.at[1, k], r_q.at[1, k], z=lax.rem(z + k, NZ))
-        cp.start()
-        sends.append(cp)
+
+    def plane_copy(half, phase, e, f, sender):
+        first, second = (0, 1) if half == 0 else (1, 0)
+        off = [0, 0]
+        if phase:
+            off[first] -= f
+        if not sender:
+            off[second if phase else first] -= e
+        ox, oy = lax.rem(x + off[0] % 4, NX), lax.rem(y + off[1] % 4, NY)
+        rows = pl.ds(half * HALF, HALF)
+        dst = PT.at[ox // 2, oy * 2 + lax.rem(ox, 2), rows]
+        src = p_ref.at[rows] if sender and f == 0 else dst
+        at = (half, phase * (f + 1), e)
+        return copy(src, dst, s_p.at[at], r_p.at[at], **along(second if phase else first, e))
+
+    def ring_copy(group, hop, back, e, rows, number, sender):
+        oz = lax.rem(z + (16 - back - (0 if sender else e)) % NZ, NZ)
+        h = xh if group == 0 else 1 - xh
+        dst = Q.at[h, oz * 2 + c, rows]
+        src = dst
+        if sender and back == 0 and group == 0:
+            src = q_ref.at[own_rows]
+        at = (group, number)
+        return copy(src, dst, s_q.at[at], r_q.at[at], **along(2, e % NZ))
+
+    whole, low, high = pl.ds(0, HALF), pl.ds(0, 32), pl.ds(32, 32)
+    hops = [(0, 0, 2, whole), (0, 0, -2, whole), (0, 0, 1, whole), (0, 0, -1, whole),
+            (1, 2, 2, low), (1, -2, -2, high), (1, 2, 1, whole), (1, -2, -1, whole)]
+
+    def ring(group, n, sender):
+        return ring_copy(group, *hops[n], n, sender)
+
+    def across(k, group, source):
+        h = xh if group == 0 else 1 - xh
+        oz = lax.rem(z + k, NZ)
+        dst = Q.at[h, oz * 2 + (c if source else 1 - c)]
+        src = q_ref.at[own_rows] if source and isinstance(k, int) and k == 0 and group == 0 else Q.at[h, oz * 2 + c]
+        return copy(src, dst, s_d.at[k, group], r_d.at[k, group], c=1 - c)
+
+    def ring_take(group, n, *ks):
+        for m in n:
+            ring(group, m, False).wait_recv()
+        for k in ks:
+            start(across(k, group, True))
+
+    start(copy(q_ref.at[other_rows], Q.at[xh, slot_q], s_xq, r_xq, **along(0, 2)))
+    for e in (2, 1, 3):
+        for half in range(2):
+            start(plane_copy(half, 0, e, 0, True))
+    for n in range(4):
+        start(ring(0, n, True))
+    for e in (2, 1, 3):
+        for half in range(2):
+            start(plane_copy(half, 1, e, 0, True))
+    start(across(0, 0, True))
     Q[xh, slot_q] = q_ref[own_rows, :]
     PT[xh, slot_p] = p_ref[...]
-    cp = copy(q_ref.at[own_rows], Q.at[xh, slot_q], s_d.at[0], r_d.at[0], c=1 - c)
-    cp.start()
-    sends.append(cp)
-    cp = copy(Q.at[1 - xh, slot_q], Q.at[1 - xh, slot_q], s_d.at[8], r_d.at[8], c=1 - c)
-    cp.start()
-    sends.append(cp)
 
     for s in range(16):
         line = (s // 2) * 16 + y * 4 + xl * 2 + s % 2
         tmp[...] = to_rows(pos_ref[pl.ds(line, 1), :])
         posc[s * HALF : (s + 1) * HALF] = tmp[own_rows, :]
 
-    for k in range(1, 8):
-        fz = lax.rem(z + 8 - k, NZ)
-        for h, part in ((0, xh), (1, 1 - xh)):
-            copy(Q.at[part, slot_q], Q.at[part, fz * 2 + c], s_q.at[h, k], r_q.at[h, k], z=fz).wait_recv()
-        cp = copy(Q.at[:, fz * 2 + c], Q.at[:, fz * 2 + c], s_d.at[k], r_d.at[k], c=1 - c)
-        cp.start()
-        sends.append(cp)
-    for k in range(1, 16):
-        fx, fy = plane_from(k)
-        copy(p_ref, PT.at[fx // 2, fy * 2 + lax.rem(fx, 2)], s_p.at[k], r_p.at[k], c=1 - c).wait_recv()
-    for k in range(0, 8):
-        fz = lax.rem(z + 8 - k, NZ)
-        if k == 0:
-            copy(q_ref.at[own_rows], Q.at[xh, z * 2 + 1 - c], s_d.at[0], r_d.at[0], c=1 - c).wait_recv()
-            copy(q_ref.at[own_rows], Q.at[1 - xh, z * 2 + 1 - c], s_d.at[8], r_d.at[8], c=1 - c).wait_recv()
-        else:
-            copy(Q.at[:, slot_q], Q.at[:, fz * 2 + 1 - c], s_d.at[k], r_d.at[k], c=1 - c).wait_recv()
-
-    def score(i, carry):
+    def plane_pass(f):
+        for half in range(2):
+            plane_copy(half, 0, f, 0, False).wait_recv()
+            for e in (2, 1, 3):
+                start(plane_copy(half, 1, e, f, True))
+
+    plane_pass(1)
+    plane_pass(3)
+    copy(q_ref.at[own_rows], Q.at[1 - xh, slot_q], s_xq, r_xq, **along(0, 2)).wait_recv()
+    for n in range(4):
+        start(ring(1, n, True))
+    start(across(0, 1, True))
+    plane_pass(2)
+    ring_take(0, (0,), 6)
+    start(ring(0, 4, True))
+    start(ring(0, 6, True))
+    ring_take(0, (1,), 2)
+    start(ring(0, 5, True))
+    start(ring(0, 7, True))
+    ring_take(0, (2,), 7)
+    ring_take(0, (3,), 1)
+    ring_take(1, (0,), 6)
+    start(ring(1, 4, True))
+    start(ring(1, 6, True))
+    ring_take(1, (1,), 2)
+    start(ring(1, 5, True))
+    start(ring(1, 7, True))
+    ring_take(1, (2,), 7)
+    ring_take(1, (3,), 1)
+    for half in range(2):
+        for f in range(4):
+            for e in (1, 2, 3):
+                plane_copy(half, 1, e, f, False).wait_recv()
+    ring_take(0, (6,), 5)
+    ring_take(0, (7,), 3)
+    ring_take(0, (4, 5), 4)
+
+    def score(n, carry):
+        k = lax.rem(lax.select(lax.rem(n, 2) == 1, (n + 1) // 2, NZ - n // 2), NZ)
+        i = lax.rem(z + k, NZ)
+        for group in range(2):
+            across(k, group, False).wait_recv()
         rows = pl.ds(pl.multiple_of(i * 128, 128), 128)
         part = [
             nt(Q[h, pl.ds(i * 2, 2)].reshape(128, WIDE), PT[h].reshape(TILE, WIDE))
@@ -169,11 +221,15 @@
         total = jnp.sum(jnp.exp2(s - high), axis=1, keepdims=True)
         rown[pl.ds(i, 1)] = to_lanes(high + jnp.log(total) * LOG2E)
         chigh = jnp.max(s, axis=0, keepdims=True)
-        cmax[pl.ds(i, 1)] = chigh
-        csum[pl.ds(i, 1)] = jnp.sum(jnp.exp2(s - chigh), axis=0, keepdims=True)
+        cmax[pl.ds(n, 1)] = chigh
+        csum[pl.ds(n, 1)] = jnp.sum(jnp.exp2(s - chigh), axis=0, keepdims=True)
         return carry
 
-    lax.fori_loop(0, 8, score, 0)
+    lax.fori_loop(0, 3, score, 0)
+    ring_take(1, (6,), 5)
+    ring_take(1, (7,), 3)
+    ring_take(1, (4, 5), 4)
+    lax.fori_loop(3, 8, score, 0)
     chigh = jnp.max(cmax[...], axis=0, keepdims=True)
     ctotal = jnp.sum(csum[...] * jnp.exp2(cmax[...] - chigh), axis=0, keepdims=True)
     cnorm = chigh + jnp.log(ctotal) * LOG2E
@@ -304,9 +360,9 @@
             pltpu.VMEM((16, ROWS + 16, WIDE), i16),
             pltpu.VMEM((16, ROWS + 16, WIDE), i16),
             dma, dma,
-            dma((16,)), dma((16,)),
+            dma((2, 5, 4)), dma((2, 5, 4)),
             dma((2, 8)), dma((2, 8)),
-            dma((9,)), dma((9,)),
+            dma((8, 2)), dma((8, 2)),
             dma((16,)), dma((16,)),
             dma((16,)), dma((16,)),
             dma((8,)), dma((8,)),

time: 71.2 us -> 64.9 us (0.912)
  Pallas kernels: 67.7 us -> 61.8 us
    pallas_call x1, Pallas kernels: 67.7 us -> 61.8 us  [local(): pl.pallas_call(kernel, out_shape=(out, out), in_specs=[vmem] * 3, out_spe...]
where the time goes in v3:
time: 64.9 us; the launch traced here: 64.7 us
  Pallas kernels  61.8 us (95%)
  local copies, waits for them, and re-layouts  2.26 us (3%)
  between operations  0.65 us (1%)
    pallas_call x1, Pallas kernels, local(): pl.pallas_call(kernel, out_shape=(out, out), in_specs=[vmem] * 3, out_spe...  61.8 us
    unnamed x4, local copies, waits for them, and re-layouts  2.26 us

profile of v3, /device:TPU:1, one launch (start us, length us, event | category | flops | bytes accessed | tf_op | source)
XLA Modules:
  0.0 64.7 jit_solution(14208187619648703353)
XLA Ops:
  0.6 61.8 %shard_map.50 = (f32[128,256]{1,0:T(8,128)}, f32[128,256]{1,0:T(8,128)}) custom-call(bf16[128,256]{1,0:T(8,128)(2,1)} %q_ref.1, bf16[128,256]{1,0:T(8,128)(2,1)} %p_ref.1, s32[128,128]{1,0:T(8,128)} %bitcast.1), custom_call_target="tpu_custom_call" | custom-call | tf_op jit(solution)/shard_map/pallas_call | solution.py:337
  62.4 0.0 copy-start
  62.4 1.6 %copy.7 = f32[128,256]{1,0:T(8,128)} copy(f32[128,256]{1,0:T(8,128)} %get-tuple-element.4) | data formatting | bytes 262144
  64.0 0.0 copy-done
  64.0 0.7 %copy.8 = f32[128,256]{1,0:T(8,128)} copy(f32[128,256]{1,0:T(8,128)S(1)} %copy-done) | data formatting | bytes 262144
Async XLA Ops:
  62.4 1.6 %copy-start = (f32[128,256]{1,0:T(8,128)S(1)}, f32[128,256]{1,0:T(8,128)}, u32[]{:S(2)}) copy-start(f32[128,256]{1,0:T(8,128)} %get-tuple-element.5) | copy-start | bytes 393220

commit v4 on v3

--- a/solution.py
+++ b/solution.py
@@ -16,25 +16,28 @@
 HALF = 64
 WIDE = 256
 TILE = 1024
+FIRST = 64
 STEP = 32000.0
 LOG2E = 1.4426950408889634
 LN2 = 0.6931471805599453
 
 
-def encode(x):
+def put(ref, x):
+    rows = x.shape[0]
     top = jnp.max(jnp.abs(x), axis=0, keepdims=True)
     power = jnp.clip(jnp.floor(jnp.log(top) * LOG2E) + 1.0, -120.0, 120.0)
-    value = jnp.round(x * (STEP * jnp.exp2(-power)))
-    power = jnp.broadcast_to(power, (16, x.shape[1]))
-    return (
-        value.astype(jnp.int32).astype(jnp.int16),
-        power.astype(jnp.int32).astype(jnp.int16),
-    )
-
-
-def decode(value, power):
-    unit = jnp.exp2(power.astype(jnp.int32).astype(jnp.float32)[:1]) * (1.0 / STEP)
-    return value.astype(jnp.int32).astype(jnp.float32) * unit
+    value = jnp.round(x * (STEP * jnp.exp2(-power))).astype(jnp.int32).astype(jnp.int16)
+    ref[0:rows] = value[:, :128]
+    ref[rows : 2 * rows] = value[:, 128:]
+    both = [jnp.broadcast_to(power[:, at : at + 128], (8, 128)) for at in (0, 128)]
+    ref[2 * rows :] = jnp.concatenate(both, axis=0).astype(jnp.int32).astype(jnp.int16)
+
+
+def take(ref):
+    rows = (ref.shape[0] - 16) // 2
+    unit = jnp.exp2(ref[2 * rows :].astype(jnp.int32).astype(jnp.float32)) * (1.0 / STEP)
+    value = ref[0 : 2 * rows].astype(jnp.int32).astype(jnp.float32)
+    return jnp.concatenate([value[:rows] * unit[0:1], value[rows:] * unit[8:9]], axis=1)
 
 
 def to_lanes(column):
@@ -61,7 +64,7 @@
 def kernel(
     q_ref, p_ref, pos_ref, gq_ref, gp_ref,
     Q, PT, S, W, posc, tmp, cmax, csum, rstat, cstat, rown, cown, rfin,
-    XQ, GQ, SQ, RQ, SP, RP,
+    XQ, GQ, SQ, RQ, OWN1, OWN2, SP1, SP2, RP1, RP2, SS1, SS2, RS1, RS2,
     s_xq, r_xq, s_p, r_p, s_q, r_q, s_d, r_d, s_rs, r_rs, s_cs, r_cs,
     s_x, r_x, s_gp, r_gp, s_gq, r_gq,
 ):
@@ -267,64 +270,117 @@
 
     lax.fori_loop(0, 8, weigh, 0)
 
-    for k in range(8):
-        tz = lax.rem(z + k, NZ)
-        rows = pl.ds(pl.multiple_of(tz * 128, 128), 128)
+    def query_product(k):
+        rows = pl.ds(pl.multiple_of(lax.rem(z + k, NZ) * 128, 128), 128)
         for h in range(2):
             part = jnp.dot(W[rows, :], PT[h].reshape(TILE, WIDE), preferred_element_type=jnp.float32)
-            tmp2 = part.reshape(2, HALF, WIDE)
-            GQ[k, 0, h] = tmp2[0]
-            GQ[k, 1, h] = tmp2[1]
-        cp = copy(GQ.at[k, 1 - c], XQ.at[k], s_x.at[k], r_x.at[k], c=1 - c)
-        cp.start()
-        sends.append(cp)
-
-    def send_queries(k):
-        copy(GQ.at[k, 1 - c], XQ.at[k], s_x.at[k], r_x.at[k], c=1 - c).wait_recv()
-        tz = lax.rem(z + k, NZ)
-        for d in range(2):
-            h = lax.rem(xh + d, 2)
-            value, power = encode(GQ[k, c, h] + XQ[k, h])
-            if k == 0 and d == 0:
-                RQ[0, 0, 0:HALF] = value
-                RQ[0, 0, HALF:] = power
-                continue
-            SQ[k, d, 0:HALF] = value
-            SQ[k, d, HALF:] = power
-            cp = copy(SQ.at[k, d], RQ.at[k, d], s_gq.at[k, d], r_gq.at[k, d], z=tz, xh=h)
-            cp.start()
-            sends.append(cp)
-
-    order = [k for k in range(1, 16)] + [0]
-    for n, k in enumerate(order):
-        tx, ty, where = plane(k)
+            part = part.reshape(2, HALF, WIDE)
+            GQ[k, 0, h] = part[0]
+            GQ[k, 1, h] = part[1]
+        start(swap(k))
+
+    def swap(k):
+        return copy(GQ.at[k, 1 - c], XQ.at[k], s_x.at[k], r_x.at[k], c=1 - c)
+
+    def side(d):
+        return xh if d == 0 else 1 - xh
+
+    def query_sum(k, d):
+        return GQ[k, c, side(d)] + XQ[k, side(d)]
+
+    legs = [(4, 0, 2), (4, 1, -2), (3, 0, 1), (3, 1, 1), (5, 0, -1), (5, 1, -1),
+            (2, 0, 2), (2, 1, 2), (6, 0, -2), (6, 1, -2), (1, 0, 1), (1, 1, 1), (7, 0, -1), (7, 1, -1), (0, 1, 0)]
+
+    def leg(n):
+        k, d, e = legs[n]
+        where = along(2, e % NZ) if e else {}
+        if n >= 6 and d:
+            where["xh"] = 1 - xh
+        return copy(SQ.at[n], RQ.at[n], s_gq.at[n], r_gq.at[n], **where)
+
+    def query_send(k):
+        swap(k).wait_recv()
+        for n, (kk, d, e) in enumerate(legs):
+            if kk == k:
+                x_ = query_sum(k, d)
+                for m in {2: {0: (0, 2), 1: (3,)}, 6: {0: (4,), 1: (1, 5)}}.get(k, {}).get(d, ()):
+                    leg(m).wait_recv()
+                    x_ = x_ + take(RQ.at[m])
+                put(SQ.at[n], x_)
+                start(leg(n))
+
+    split = (pl.ds(0, FIRST), pl.ds(FIRST, ROWS - FIRST))
+    own, sp, rp, sp2, rp2 = (OWN1, OWN2), (SP1, SP2), (RP1, RP2), (SS1, SS2), (RS1, RS2)
+
+    def plane_leg(half, e, t):
+        at = (half, e - 1, t)
+        return copy(sp[half].at[e - 1, t], rp[half].at[e - 1, t], s_gp.at[at], r_gp.at[at], **along(half, e))
+
+    def plane_last(half, t):
+        at = (half, 3, t)
+        return copy(sp2[half].at[t - 1], rp2[half].at[t - 1], s_gp.at[at], r_gp.at[at], **along(1 - half, t))
+
+    def passage_product(a, b):
+        tx, ty = lax.rem(x + a, NX), lax.rem(y + b, NY)
         cols = pl.ds(pl.multiple_of((ty * 2 + lax.rem(tx, 2)) * 128, 128), 128)
-        value, power = encode(tn(W[:, cols], Q[tx // 2].reshape(TILE, WIDE)))
-        if k == 0:
-            RP[0, 0:ROWS] = value
-            RP[0, ROWS:] = power
-        else:
-            SP[k, 0:ROWS] = value
-            SP[k, ROWS:] = power
-            cp = copy(SP.at[k], RP.at[k], s_gp.at[k], r_gp.at[k], **where)
-            cp.start()
-            sends.append(cp)
-        if n % 2 == 1:
-            send_queries((n // 2 + 1) % 8)
-
-    total = jnp.zeros((ROWS, WIDE), jnp.float32)
-    for k in range(16):
-        if k:
-            copy(SP.at[k], RP.at[k], s_gp.at[k], r_gp.at[k], **plane(k)[2]).wait_recv()
-        total = total + decode(RP[k, 0:ROWS], RP[k, ROWS:])
-    gp_ref[...] = total * factor
-    for d in range(2):
-        total = jnp.zeros((HALF, WIDE), jnp.float32)
-        for k in range(8):
-            if k or d:
-                copy(SQ.at[k, d], RQ.at[k, d], s_gq.at[k, d], r_gq.at[k, d], z=lax.rem(z + k, NZ)).wait_recv()
-            total = total + decode(RQ[k, d, 0:HALF], RQ[k, d, HALF:])
-        gq_ref[(own_rows, other_rows)[d], :] = total * factor
+        part = tn(W[:, cols], Q[tx // 2].reshape(TILE, WIDE))
+        for half, e, t in ((0, a, b), (1, b, a)):
+            rows = part[0:FIRST] if half == 0 else part[FIRST:]
+            if e:
+                put(sp[half].at[e - 1, t], rows)
+                start(plane_leg(half, e, t))
+            else:
+                own[half][t] = rows
+
+    def plane_sum(half, t):
+        total = own[half][t]
+        for e in (1, 3, 2):
+            plane_leg(half, e, t).wait_recv()
+            total = total + take(rp[half].at[e - 1, t])
+        return total
+
+    def plane_send(t):
+        for half in range(2):
+            put(sp2[half].at[t - 1], plane_sum(half, t))
+            start(plane_last(half, t))
+
+    for k in (4, 3, 5):
+        query_product(k)
+    for a, b in ((2, 2), (1, 2), (2, 1)):
+        passage_product(a, b)
+    for k in (4, 3, 5):
+        query_send(k)
+    for a, b in ((3, 2), (2, 3), (0, 2), (2, 0)):
+        passage_product(a, b)
+    for k in (2, 6, 1, 7, 0):
+        query_product(k)
+    for a, b in ((1, 1), (3, 1), (1, 3), (3, 3)):
+        passage_product(a, b)
+    for k in (1, 7, 0):
+        query_send(k)
+    for a, b in ((0, 1), (1, 0), (0, 3), (3, 0), (0, 0)):
+        passage_product(a, b)
+    plane_send(2)
+    for k in (2, 6):
+        query_send(k)
+    plane_send(1)
+    plane_send(3)
+    for half in range(2):
+        total = plane_sum(half, 0)
+        for t in (2, 1, 3):
+            plane_last(half, t).wait_recv()
+            total = total + take(rp2[half].at[t - 1])
+        gp_ref[split[half], :] = total * factor
+    total = query_sum(0, 0)
+    for n in (10, 12, 6, 8):
+        leg(n).wait_recv()
+        total = total + take(RQ.at[n])
+    gq_ref[own_rows, :] = total * factor
+    total = jnp.zeros((HALF, WIDE), jnp.float32)
+    for n in (14, 11, 13, 7, 9):
+        leg(n).wait_recv()
+        total = total + take(RQ.at[n])
+    gq_ref[other_rows, :] = total * factor
     for cp in sends:
         cp.wait_send()
 
@@ -333,6 +389,7 @@
     dma = pltpu.SemaphoreType.DMA
     vmem = pl.BlockSpec(memory_space=pltpu.VMEM)
     out = jax.ShapeDtypeStruct((ROWS, WIDE), jnp.float32)
+    parts = (FIRST, ROWS - FIRST)
     bf16, f32, i16 = jnp.bfloat16, jnp.float32, jnp.int16
     return pl.pallas_call(
         kernel,
@@ -355,10 +412,11 @@
             pltpu.VMEM((8, 128), f32),
             pltpu.VMEM((8, 2, HALF, WIDE), f32),
             pltpu.VMEM((8, 2, 2, HALF, WIDE), f32),
-            pltpu.VMEM((8, 2, HALF + 16, WIDE), i16),
-            pltpu.VMEM((8, 2, HALF + 16, WIDE), i16),
-            pltpu.VMEM((16, ROWS + 16, WIDE), i16),
-            pltpu.VMEM((16, ROWS + 16, WIDE), i16),
+            pltpu.VMEM((15, 2 * HALF + 16, 128), i16),
+            pltpu.VMEM((15, 2 * HALF + 16, 128), i16),
+            *(pltpu.VMEM((4, r, WIDE), f32) for r in parts),
+            *(pltpu.VMEM((3, 4, 2 * r + 16, 128), i16) for _ in range(2) for r in parts),
+            *(pltpu.VMEM((3, 2 * r + 16, 128), i16) for _ in range(2) for r in parts),
             dma, dma,
             dma((2, 5, 4)), dma((2, 5, 4)),
             dma((2, 8)), dma((2, 8)),
@@ -366,8 +424,8 @@
             dma((16,)), dma((16,)),
             dma((16,)), dma((16,)),
             dma((8,)), dma((8,)),
-            dma((16,)), dma((16,)),
-            dma((8, 2)), dma((8, 2)),
+            dma((2, 4, 4)), dma((2, 4, 4)),
+            dma((15,)), dma((15,)),
         ],
         compiler_params=pltpu.CompilerParams(
             collective_id=0, has_side_effects=True, vmem_limit_bytes=60 * 1024 * 1024

time: 64.9 us -> 56.8 us (0.88)
  Pallas kernels: 61.8 us -> 53.7 us
    pallas_call x1, Pallas kernels: 61.8 us -> 53.7 us  [local(): pl.pallas_call(kernel, out_shape=(out, out), in_specs=[vmem] * 3, out_spe...]
where the time goes in v4:
time: 56.8 us; the launch traced here: 56.6 us
  Pallas kernels  53.7 us (95%)
  local copies, waits for them, and re-layouts  2.26 us (4%)
  between operations  0.65 us (1%)
    pallas_call x1, Pallas kernels, local(): pl.pallas_call(kernel, out_shape=(out, out), in_specs=[vmem] * 3, out_spe...  53.7 us
    unnamed x4, local copies, waits for them, and re-layouts  2.26 us

profile of v4, /device:TPU:1, one launch (start us, length us, event | category | flops | bytes accessed | tf_op | source)
XLA Modules:
  0.0 56.6 jit_solution(9639727753917745367)
XLA Ops:
  0.6 53.7 %shard_map.50 = (f32[128,256]{1,0:T(8,128)}, f32[128,256]{1,0:T(8,128)}) custom-call(bf16[128,256]{1,0:T(8,128)(2,1)} %q_ref.1, bf16[128,256]{1,0:T(8,128)(2,1)} %p_ref.1, s32[128,128]{1,0:T(8,128)} %bitcast.1), custom_call_target="tpu_custom_call" | custom-call | tf_op jit(solution)/shard_map/pallas_call | solution.py:394
  54.4 0.0 copy-start
  54.4 1.6 %copy.7 = f32[128,256]{1,0:T(8,128)} copy(f32[128,256]{1,0:T(8,128)} %get-tuple-element.4) | data formatting | bytes 262144
  56.0 0.0 copy-done
  56.0 0.7 %copy.8 = f32[128,256]{1,0:T(8,128)} copy(f32[128,256]{1,0:T(8,128)S(1)} %copy-done) | data formatting | bytes 262144
Async XLA Ops:
  54.4 1.6 %copy-start = (f32[128,256]{1,0:T(8,128)S(1)}, f32[128,256]{1,0:T(8,128)}, u32[]{:S(2)}) copy-start(f32[128,256]{1,0:T(8,128)} %get-tuple-element.5) | copy-start | bytes 393220

commit v5 on v4

--- a/solution.py
+++ b/solution.py
@@ -62,10 +62,10 @@
 
 
 def kernel(
-    q_ref, p_ref, pos_ref, gq_ref, gp_ref,
+    q_hbm, p_hbm, pos_hbm, gq_ref, gp_ref, q_ref, p_ref, pos_ref,
     Q, PT, S, W, posc, tmp, cmax, csum, rstat, cstat, rown, cown, rfin,
     XQ, GQ, SQ, RQ, OWN1, OWN2, SP1, SP2, RP1, RP2, SS1, SS2, RS1, RS2,
-    s_xq, r_xq, s_p, r_p, s_q, r_q, s_d, r_d, s_rs, r_rs, s_cs, r_cs,
+    s_in, s_xq, r_xq, s_p, r_p, s_q, r_q, s_d, r_d, s_rs, r_rs, s_cs, r_cs,
     s_x, r_x, s_gp, r_gp, s_gq, r_gq,
 ):
     z, y, xl, c, xh = (lax.axis_index(a) for a in AXES)
@@ -97,6 +97,14 @@
     near += [along(2, e) for e in (1, 7, 2, 6)] + [{"c": 1 - c}]
     for where in near:
         pl.semaphore_signal(barrier, inc=1, device_id=where, device_id_type=MESH)
+    loads = [
+        pltpu.make_async_copy(src, dst, s_in.at[n])
+        for n, (src, dst) in enumerate(((q_hbm, q_ref), (p_hbm, p_ref), (pos_hbm, pos_ref)))
+    ]
+    for load in loads:
+        load.start()
+    for load in loads:
+        load.wait()
     pl.semaphore_wait(barrier, len(near))
 
     slot_q = z * 2 + c
@@ -344,27 +352,26 @@
             put(sp2[half].at[t - 1], plane_sum(half, t))
             start(plane_last(half, t))
 
-    for k in (4, 3, 5):
+    for k in (4, 3, 5,):
         query_product(k)
-    for a, b in ((2, 2), (1, 2), (2, 1)):
+    for a, b in ((2, 2), (1, 2), (2, 1),):
         passage_product(a, b)
-    for k in (4, 3, 5):
+    for k in (4, 3, 5,):
         query_send(k)
-    for a, b in ((3, 2), (2, 3), (0, 2), (2, 0)):
+    for a, b in ((3, 2), (2, 3), (0, 2), (2, 0),):
         passage_product(a, b)
-    for k in (2, 6, 1, 7, 0):
+    for k in (2, 6, 1, 7, 0,):
         query_product(k)
-    for a, b in ((1, 1), (3, 1), (1, 3), (3, 3)):
+    for a, b in ((1, 1), (3, 1), (1, 3), (3, 3),):
         passage_product(a, b)
-    for k in (1, 7, 0):
+    for k in (1, 7, 0,):
         query_send(k)
-    for a, b in ((0, 1), (1, 0), (0, 3), (3, 0), (0, 0)):
+    for a, b in ((0, 1), (1, 0), (0, 3), (3, 0), (0, 0),):
         passage_product(a, b)
-    plane_send(2)
-    for k in (2, 6):
+    for k in (2, 6,):
         query_send(k)
-    plane_send(1)
-    plane_send(3)
+    for k in (2, 1, 3,):
+        plane_send(k)
     for half in range(2):
         total = plane_sum(half, 0)
         for t in (2, 1, 3):
@@ -388,15 +395,17 @@
 def local(queries, passages, positives):
     dma = pltpu.SemaphoreType.DMA
     vmem = pl.BlockSpec(memory_space=pltpu.VMEM)
-    out = jax.ShapeDtypeStruct((ROWS, WIDE), jnp.float32)
+    out = pltpu.VMEM((ROWS, WIDE), jnp.float32)
     parts = (FIRST, ROWS - FIRST)
     bf16, f32, i16 = jnp.bfloat16, jnp.float32, jnp.int16
     return pl.pallas_call(
         kernel,
         out_shape=(out, out),
-        in_specs=[vmem] * 3,
+        in_specs=[pl.BlockSpec(memory_space=pl.ANY)] * 3,
         out_specs=(vmem, vmem),
         scratch_shapes=[
+            *(pltpu.VMEM((ROWS, WIDE), bf16) for _ in range(2)),
+            pltpu.VMEM((128, 128), jnp.int32),
             pltpu.VMEM((2, 16, HALF, WIDE), bf16),
             pltpu.VMEM((2, 8, ROWS, WIDE), bf16),
             pltpu.VMEM((TILE, TILE), f32),
@@ -417,6 +426,7 @@
             *(pltpu.VMEM((4, r, WIDE), f32) for r in parts),
             *(pltpu.VMEM((3, 4, 2 * r + 16, 128), i16) for _ in range(2) for r in parts),
             *(pltpu.VMEM((3, 2 * r + 16, 128), i16) for _ in range(2) for r in parts),
+            dma((3,)),
             dma, dma,
             dma((2, 5, 4)), dma((2, 5, 4)),
             dma((2, 8)), dma((2, 8)),

time: 56.8 us -> 54.4 us (0.958)
  Pallas kernels: 53.7 us -> 52.3 us
  local copies, waits for them, and re-layouts: 2.26 us -> 1.31 us
    pallas_call x1, Pallas kernels: 53.7 us -> 52.3 us  [local(): pl.pallas_call(kernel, out_shape=(out, out), in_specs=[pl.BlockSpec(memor...]
    unnamed x4 -> x2, local copies, waits for them, and re-layouts: 2.26 us -> 1.31 us
where the time goes in v5:
time: 54.4 us; the launch traced here: 54.2 us
  Pallas kernels  52.3 us (96%)
  local copies, waits for them, and re-layouts  1.31 us (2%)
  between operations  0.64 us (1%)
    pallas_call x1, Pallas kernels, local(): pl.pallas_call(kernel, out_shape=(out, out), in_specs=[pl.BlockSpec(memor...  52.3 us
    unnamed x2, local copies, waits for them, and re-layouts  1.31 us

profile of v5, /device:TPU:1, one launch (start us, length us, event | category | flops | bytes accessed | tf_op | source)
XLA Modules:
  0.0 54.2 jit_solution(3182492022158127004)
XLA Ops:
  0.6 52.3 %shard_map.50 = (f32[128,256]{1,0:T(8,128)S(1)}, f32[128,256]{1,0:T(8,128)S(1)}) custom-call(bf16[128,256]{1,0:T(8,128)(2,1)} %q_hbm.1, bf16[128,256]{1,0:T(8,128)(2,1)} %p_hbm.1, s32[128,128]{1,0:T(8,128)} %bitcast.1), custom_call_target="tpu_custom_call" | custom-call | tf_op jit(solution)/shard_map/pallas_call | solution.py:401
  52.9 0.7 %copy.7 = f32[128,256]{1,0:T(8,128)} copy(f32[128,256]{1,0:T(8,128)S(1)} %get-tuple-element.2) | data formatting | bytes 262144
  53.6 0.7 %copy.8 = f32[128,256]{1,0:T(8,128)} copy(f32[128,256]{1,0:T(8,128)S(1)} %get-tuple-element.3) | data formatting | bytes 262144

commit v6 on v5

--- a/solution.py
+++ b/solution.py
@@ -16,6 +16,9 @@
 HALF = 64
 WIDE = 256
 TILE = 1024
+ORDER = (0, 1, 7, 2, 6, 3, 5, 4)
+POS = tuple(ORDER.index(k) for k in range(8))
+SPLIT = 4
 FIRST = 64
 STEP = 32000.0
 LOG2E = 1.4426950408889634
@@ -107,7 +110,6 @@
         load.wait()
     pl.semaphore_wait(barrier, len(near))
 
-    slot_q = z * 2 + c
     slot_p = y * 2 + xl
     own_rows = pl.ds(pl.multiple_of(xh * HALF, HALF), HALF)
     other_rows = pl.ds(pl.multiple_of((1 - xh) * HALF, HALF), HALF)
@@ -132,10 +134,9 @@
         return copy(src, dst, s_p.at[at], r_p.at[at], **along(second if phase else first, e))
 
     def ring_copy(group, hop, back, e, rows, number, sender):
-        oz = lax.rem(z + (16 - back - (0 if sender else e)) % NZ, NZ)
         h = xh if group == 0 else 1 - xh
-        dst = Q.at[h, oz * 2 + c, rows]
-        src = dst
+        src = Q.at[h, POS[-back % NZ], c, rows]
+        dst = Q.at[h, POS[(-back - e) % NZ], c, rows]
         if sender and back == 0 and group == 0:
             src = q_ref.at[own_rows]
         at = (group, number)
@@ -150,9 +151,8 @@
 
     def across(k, group, source):
         h = xh if group == 0 else 1 - xh
-        oz = lax.rem(z + k, NZ)
-        dst = Q.at[h, oz * 2 + (c if source else 1 - c)]
-        src = q_ref.at[own_rows] if source and isinstance(k, int) and k == 0 and group == 0 else Q.at[h, oz * 2 + c]
+        src = q_ref.at[own_rows] if k == 0 and group == 0 else Q.at[h, POS[k], c]
+        dst = Q.at[h, POS[k], c if source else 1 - c]
         return copy(src, dst, s_d.at[k, group], r_d.at[k, group], c=1 - c)
 
     def ring_take(group, n, *ks):
@@ -161,7 +161,7 @@
         for k in ks:
             start(across(k, group, True))
 
-    start(copy(q_ref.at[other_rows], Q.at[xh, slot_q], s_xq, r_xq, **along(0, 2)))
+    start(copy(q_ref.at[other_rows], Q.at[xh, 0, c], s_xq, r_xq, **along(0, 2)))
     for e in (2, 1, 3):
         for half in range(2):
             start(plane_copy(half, 0, e, 0, True))
@@ -171,11 +171,11 @@
         for half in range(2):
             start(plane_copy(half, 1, e, 0, True))
     start(across(0, 0, True))
-    Q[xh, slot_q] = q_ref[own_rows, :]
+    Q[xh, 0, c] = q_ref[own_rows, :]
     PT[xh, slot_p] = p_ref[...]
 
     for s in range(16):
-        line = (s // 2) * 16 + y * 4 + xl * 2 + s % 2
+        line = lax.rem(z + ORDER[s // 2], NZ) * 16 + y * 4 + xl * 2 + s % 2
         tmp[...] = to_rows(pos_ref[pl.ds(line, 1), :])
         posc[s * HALF : (s + 1) * HALF] = tmp[own_rows, :]
 
@@ -187,7 +187,7 @@
 
     plane_pass(1)
     plane_pass(3)
-    copy(q_ref.at[own_rows], Q.at[1 - xh, slot_q], s_xq, r_xq, **along(0, 2)).wait_recv()
+    copy(q_ref.at[own_rows], Q.at[1 - xh, 0, c], s_xq, r_xq, **along(0, 2)).wait_recv()
     for n in range(4):
         start(ring(1, n, True))
     start(across(0, 1, True))
@@ -216,31 +216,38 @@
     ring_take(0, (7,), 3)
     ring_take(0, (4, 5), 4)
 
-    def score(n, carry):
-        k = lax.rem(lax.select(lax.rem(n, 2) == 1, (n + 1) // 2, NZ - n // 2), NZ)
-        i = lax.rem(z + k, NZ)
-        for group in range(2):
-            across(k, group, False).wait_recv()
-        rows = pl.ds(pl.multiple_of(i * 128, 128), 128)
+    def tile_z(n):
+        odd = lax.rem(n, 2) == 1
+        k = jnp.where(odd, (n + 1) // 2, NZ - n // 2)
+        return lax.rem(z + k, NZ)
+
+    def score_dots(first, last):
+        for n in range(first, last):
+            for group in range(2):
+                across(ORDER[n], group, False).wait_recv()
         part = [
-            nt(Q[h, pl.ds(i * 2, 2)].reshape(128, WIDE), PT[h].reshape(TILE, WIDE))
+            nt(Q[h, first:last].reshape((last - first) * 128, WIDE), PT[h].reshape(TILE, WIDE))
             for h in range(2)
         ]
-        s = (part[0] + part[1]) * (factor * LOG2E)
-        S[rows] = s
+        S[first * 128 : last * 128] = (part[0] + part[1]) * (factor * LOG2E)
+
+    def score(n, carry):
+        s = S[pl.ds(pl.multiple_of(n * 128, 128), 128)]
         high = jnp.max(s, axis=1, keepdims=True)
         total = jnp.sum(jnp.exp2(s - high), axis=1, keepdims=True)
-        rown[pl.ds(i, 1)] = to_lanes(high + jnp.log(total) * LOG2E)
+        rown[pl.ds(tile_z(n), 1)] = to_lanes(high + jnp.log(total) * LOG2E)
         chigh = jnp.max(s, axis=0, keepdims=True)
         cmax[pl.ds(n, 1)] = chigh
         csum[pl.ds(n, 1)] = jnp.sum(jnp.exp2(s - chigh), axis=0, keepdims=True)
         return carry
 
-    lax.fori_loop(0, 3, score, 0)
+    score_dots(0, SPLIT)
+    lax.fori_loop(0, SPLIT, score, 0)
     ring_take(1, (6,), 5)
     ring_take(1, (7,), 3)
     ring_take(1, (4, 5), 4)
-    lax.fori_loop(3, 8, score, 0)
+    score_dots(SPLIT, 8)
+    lax.fori_loop(SPLIT, 8, score, 0)
     chigh = jnp.max(cmax[...], axis=0, keepdims=True)
     ctotal = jnp.sum(csum[...] * jnp.exp2(cmax[...] - chigh), axis=0, keepdims=True)
     cnorm = chigh + jnp.log(ctotal) * LOG2E
@@ -265,7 +272,7 @@
 
     def weigh(i, carry):
         rows = pl.ds(pl.multiple_of(i * 128, 128), 128)
-        rnorm = to_rows(rfin[pl.ds(i, 1), :])
+        rnorm = to_rows(rfin[pl.ds(tile_z(i), 1), :])
         for b in range(8):
             cols = slice(b * 128, (b + 1) * 128)
             s = S[rows, cols]
@@ -276,25 +283,24 @@
             W[rows, cols] = w.astype(jnp.bfloat16)
         return carry
 
-    lax.fori_loop(0, 8, weigh, 0)
-
-    def query_product(k):
-        rows = pl.ds(pl.multiple_of(lax.rem(z + k, NZ) * 128, 128), 128)
+    lax.fori_loop(5, 8, weigh, 0)
+
+    def query_products(first, last):
         for h in range(2):
-            part = jnp.dot(W[rows, :], PT[h].reshape(TILE, WIDE), preferred_element_type=jnp.float32)
-            part = part.reshape(2, HALF, WIDE)
-            GQ[k, 0, h] = part[0]
-            GQ[k, 1, h] = part[1]
-        start(swap(k))
+            part = jnp.dot(W[first * 128 : last * 128], PT[h].reshape(TILE, WIDE), preferred_element_type=jnp.float32)
+            GQ[first:last, :, h] = part.reshape(last - first, 2, HALF, WIDE)
+        for n in range(last - 1, first - 1, -1):
+            start(swap(ORDER[n]))
 
     def swap(k):
-        return copy(GQ.at[k, 1 - c], XQ.at[k], s_x.at[k], r_x.at[k], c=1 - c)
+        n = POS[k]
+        return copy(GQ.at[n, 1 - c], XQ.at[n], s_x.at[n], r_x.at[n], c=1 - c)
 
     def side(d):
         return xh if d == 0 else 1 - xh
 
     def query_sum(k, d):
-        return GQ[k, c, side(d)] + XQ[k, side(d)]
+        return GQ[POS[k], c, side(d)] + XQ[POS[k], side(d)]
 
     legs = [(4, 0, 2), (4, 1, -2), (3, 0, 1), (3, 1, 1), (5, 0, -1), (5, 1, -1),
             (2, 0, 2), (2, 1, 2), (6, 0, -2), (6, 1, -2), (1, 0, 1), (1, 1, 1), (7, 0, -1), (7, 1, -1), (0, 1, 0)]
@@ -306,16 +312,19 @@
             where["xh"] = 1 - xh
         return copy(SQ.at[n], RQ.at[n], s_gq.at[n], r_gq.at[n], **where)
 
-    def query_send(k):
-        swap(k).wait_recv()
-        for n, (kk, d, e) in enumerate(legs):
-            if kk == k:
-                x_ = query_sum(k, d)
-                for m in {2: {0: (0, 2), 1: (3,)}, 6: {0: (4,), 1: (1, 5)}}.get(k, {}).get(d, ()):
-                    leg(m).wait_recv()
-                    x_ = x_ + take(RQ.at[m])
-                put(SQ.at[n], x_)
-                start(leg(n))
+    def query_send(*units):
+        for k, d in units:
+            n = [leg_[:2] for leg_ in legs].index((k, d))
+            total = query_sum(k, d)
+            for m in {(2, 0): (2, 0), (2, 1): (3,), (6, 0): (4,), (6, 1): (5, 1)}.get((k, d), ()):
+                leg(m).wait_recv()
+                total = total + take(RQ.at[m])
+            put(SQ.at[n], total)
+            start(leg(n))
+
+    def query_swap(*ks):
+        for k in ks:
+            swap(k).wait_recv()
 
     split = (pl.ds(0, FIRST), pl.ds(FIRST, ROWS - FIRST))
     own, sp, rp, sp2, rp2 = (OWN1, OWN2), (SP1, SP2), (RP1, RP2), (SS1, SS2), (RS1, RS2)
@@ -352,24 +361,22 @@
             put(sp2[half].at[t - 1], plane_sum(half, t))
             start(plane_last(half, t))
 
-    for k in (4, 3, 5,):
-        query_product(k)
+    query_products(5, 8)
+    lax.fori_loop(0, 5, weigh, 0)
     for a, b in ((2, 2), (1, 2), (2, 1),):
         passage_product(a, b)
-    for k in (4, 3, 5,):
-        query_send(k)
+    query_swap(4, 3, 5)
+    query_send((4, 1), (4, 0), (3, 1), (5, 1), (5, 0), (3, 0))
     for a, b in ((3, 2), (2, 3), (0, 2), (2, 0),):
         passage_product(a, b)
-    for k in (2, 6, 1, 7, 0,):
-        query_product(k)
+    query_products(0, 5)
     for a, b in ((1, 1), (3, 1), (1, 3), (3, 3),):
         passage_product(a, b)
-    for k in (1, 7, 0,):
-        query_send(k)
+    query_swap(2, 6, 1, 7, 0)
+    query_send((1, 1), (7, 1), (0, 1), (1, 0), (7, 0))
     for a, b in ((0, 1), (1, 0), (0, 3), (3, 0), (0, 0),):
         passage_product(a, b)
-    for k in (2, 6,):
-        query_send(k)
+    query_send((2, 1), (6, 1), (6, 0), (2, 0))
     for k in (2, 1, 3,):
         plane_send(k)
     for half in range(2):
@@ -406,7 +413,7 @@
         scratch_shapes=[
             *(pltpu.VMEM((ROWS, WIDE), bf16) for _ in range(2)),
             pltpu.VMEM((128, 128), jnp.int32),
-            pltpu.VMEM((2, 16, HALF, WIDE), bf16),
+            pltpu.VMEM((2, 8, 2, HALF, WIDE), bf16),
             pltpu.VMEM((2, 8, ROWS, WIDE), bf16),
             pltpu.VMEM((TILE, TILE), f32),
             pltpu.VMEM((TILE, TILE), bf16),

time: 54.4 us -> 52.7 us (0.969)
  Pallas kernels: 52.3 us -> 50.7 us
    pallas_call x1, Pallas kernels: 52.3 us -> 50.7 us  [local(): pl.pallas_call(kernel, out_shape=(out, out), in_specs=[pl.BlockSpec(memor...]
where the time goes in v6:
time: 52.7 us; the launch traced here: 52.6 us
  Pallas kernels  50.7 us (96%)
  local copies, waits for them, and re-layouts  1.31 us (2%)
  between operations  0.64 us (1%)
    pallas_call x1, Pallas kernels, local(): pl.pallas_call(kernel, out_shape=(out, out), in_specs=[pl.BlockSpec(memor...  50.7 us
    unnamed x2, local copies, waits for them, and re-layouts  1.31 us

profile of v6, /device:TPU:1, one launch (start us, length us, event | category | flops | bytes accessed | tf_op | source)
XLA Modules:
  0.0 52.6 jit_solution(5417334734319617361)
XLA Ops:
  0.6 50.7 %shard_map.50 = (f32[128,256]{1,0:T(8,128)S(1)}, f32[128,256]{1,0:T(8,128)S(1)}) custom-call(bf16[128,256]{1,0:T(8,128)(2,1)} %q_hbm.1, bf16[128,256]{1,0:T(8,128)(2,1)} %p_hbm.1, s32[128,128]{1,0:T(8,128)} %bitcast.1), custom_call_target="tpu_custom_call" | custom-call | tf_op jit(solution)/shard_map/pallas_call | solution.py:408
  51.3 0.7 %copy.7 = f32[128,256]{1,0:T(8,128)} copy(f32[128,256]{1,0:T(8,128)S(1)} %get-tuple-element.2) | data formatting | bytes 262144
  52.0 0.7 %copy.8 = f32[128,256]{1,0:T(8,128)} copy(f32[128,256]{1,0:T(8,128)S(1)} %get-tuple-element.3) | data formatting | bytes 262144

commit v7 on v6

--- a/solution.py
+++ b/solution.py
@@ -185,19 +185,19 @@
             for e in (2, 1, 3):
                 start(plane_copy(half, 1, e, f, True))
 
-    plane_pass(1)
-    plane_pass(3)
     copy(q_ref.at[own_rows], Q.at[1 - xh, 0, c], s_xq, r_xq, **along(0, 2)).wait_recv()
     for n in range(4):
         start(ring(1, n, True))
     start(across(0, 1, True))
-    plane_pass(2)
+    plane_pass(1)
+    plane_pass(3)
     ring_take(0, (0,), 6)
     start(ring(0, 4, True))
     start(ring(0, 6, True))
     ring_take(0, (1,), 2)
     start(ring(0, 5, True))
     start(ring(0, 7, True))
+    plane_pass(2)
     ring_take(0, (2,), 7)
     ring_take(0, (3,), 1)
     ring_take(1, (0,), 6)
@@ -248,6 +248,8 @@
     ring_take(1, (4, 5), 4)
     score_dots(SPLIT, 8)
     lax.fori_loop(SPLIT, 8, score, 0)
+    for k in sorted(range(1, 16), key=lambda k: -min(k // 2, 8 - k // 2)):
+        start(copy(rown, rstat.at[k], s_rs.at[k], r_rs.at[k], **pillar(k)[2]))
     chigh = jnp.max(cmax[...], axis=0, keepdims=True)
     ctotal = jnp.sum(csum[...] * jnp.exp2(cmax[...] - chigh), axis=0, keepdims=True)
     cnorm = chigh + jnp.log(ctotal) * LOG2E
@@ -255,13 +257,8 @@
         cown[b : b + 1] = cnorm[:, b * 128 : (b + 1) * 128]
     rstat[0] = rown[...]
     cstat[0] = cown[...]
-    for k in range(1, 16):
-        cp = copy(rown, rstat.at[k], s_rs.at[k], r_rs.at[k], **pillar(k)[2])
-        cp.start()
-        sends.append(cp)
-        cp = copy(cown, cstat.at[k], s_cs.at[k], r_cs.at[k], **plane(k)[2])
-        cp.start()
-        sends.append(cp)
+    for k in sorted(range(1, 16), key=lambda k: -min(k % 4, -k % 4) - min(k // 4, 4 - k // 4)):
+        start(copy(cown, cstat.at[k], s_cs.at[k], r_cs.at[k], **plane(k)[2]))
     for k in range(1, 16):
         copy(rown, rstat.at[k], s_rs.at[k], r_rs.at[k], **pillar(k)[2]).wait_recv()
         copy(cown, cstat.at[k], s_cs.at[k], r_cs.at[k], **plane(k)[2]).wait_recv()
@@ -372,15 +369,19 @@
     query_products(0, 5)
     for a, b in ((1, 1), (3, 1), (1, 3), (3, 3),):
         passage_product(a, b)
-    query_swap(2, 6, 1, 7, 0)
-    query_send((1, 1), (7, 1), (0, 1), (1, 0), (7, 0))
     for a, b in ((0, 1), (1, 0), (0, 3), (3, 0), (0, 0),):
         passage_product(a, b)
-    query_send((2, 1), (6, 1), (6, 0), (2, 0))
-    for k in (2, 1, 3,):
+    query_swap(2, 6, 1, 7, 0)
+    for k in (2,):
         plane_send(k)
+    query_send((2, 1), (6, 1))
+    query_send((6, 0), (2, 0))
+    for k in (1, 3,):
+        plane_send(k)
+    query_send((1, 1), (7, 1), (0, 1), (1, 0), (7, 0))
+    totals = [plane_sum(half, 0) for half in range(2)]
     for half in range(2):
-        total = plane_sum(half, 0)
+        total = totals[half]
         for t in (2, 1, 3):
             plane_last(half, t).wait_recv()
             total = total + take(rp2[half].at[t - 1])

time: 52.7 us -> 52 us (0.987)
  Pallas kernels: 50.7 us -> 49.9 us
    pallas_call x1, Pallas kernels: 50.7 us -> 49.9 us  [local(): pl.pallas_call(kernel, out_shape=(out, out), in_specs=[pl.BlockSpec(memor...]
where the time goes in v7:
time: 52 us; the launch traced here: 51.9 us
  Pallas kernels  49.9 us (96%)
  local copies, waits for them, and re-layouts  1.31 us (3%)
  between operations  0.64 us (1%)
    pallas_call x1, Pallas kernels, local(): pl.pallas_call(kernel, out_shape=(out, out), in_specs=[pl.BlockSpec(memor...  49.9 us
    unnamed x2, local copies, waits for them, and re-layouts  1.31 us

profile of v7, /device:TPU:1, one launch (start us, length us, event | category | flops | bytes accessed | tf_op | source)
XLA Modules:
  0.0 51.9 jit_solution(6382084916048054626)
XLA Ops:
  0.6 49.9 %shard_map.50 = (f32[128,256]{1,0:T(8,128)S(1)}, f32[128,256]{1,0:T(8,128)S(1)}) custom-call(bf16[128,256]{1,0:T(8,128)(2,1)} %q_hbm.1, bf16[128,256]{1,0:T(8,128)(2,1)} %p_hbm.1, s32[128,128]{1,0:T(8,128)} %bitcast.1), custom_call_target="tpu_custom_call" | custom-call | tf_op jit(solution)/shard_map/pallas_call | solution.py:409
  50.6 0.7 %copy.7 = f32[128,256]{1,0:T(8,128)} copy(f32[128,256]{1,0:T(8,128)S(1)} %get-tuple-element.2) | data formatting | bytes 262144
  51.2 0.7 %copy.8 = f32[128,256]{1,0:T(8,128)} copy(f32[128,256]{1,0:T(8,128)S(1)} %get-tuple-element.3) | data formatting | bytes 262144

commit v8 on v7

--- a/solution.py
+++ b/solution.py
@@ -242,12 +242,12 @@
         return carry
 
     score_dots(0, SPLIT)
-    lax.fori_loop(0, SPLIT, score, 0)
+    lax.fori_loop(0, SPLIT, score, 0, unroll=2)
     ring_take(1, (6,), 5)
     ring_take(1, (7,), 3)
     ring_take(1, (4, 5), 4)
     score_dots(SPLIT, 8)
-    lax.fori_loop(SPLIT, 8, score, 0)
+    lax.fori_loop(SPLIT, 8, score, 0, unroll=2)
     for k in sorted(range(1, 16), key=lambda k: -min(k // 2, 8 - k // 2)):
         start(copy(rown, rstat.at[k], s_rs.at[k], r_rs.at[k], **pillar(k)[2]))
     chigh = jnp.max(cmax[...], axis=0, keepdims=True)

time: 52 us -> 51.5 us (level)
  no operation moved by 1% of the time
where the time goes in v8:
time: 51.5 us; the launch traced here: 51.4 us
  Pallas kernels  49.4 us (96%)
  local copies, waits for them, and re-layouts  1.31 us (3%)
  between operations  0.64 us (1%)
    pallas_call x1, Pallas kernels, local(): pl.pallas_call(kernel, out_shape=(out, out), in_specs=[pl.BlockSpec(memor...  49.4 us
    unnamed x2, local copies, waits for them, and re-layouts  1.31 us

profile of v8, /device:TPU:1, one launch (start us, length us, event | category | flops | bytes accessed | tf_op | source)
XLA Modules:
  0.0 51.4 jit_solution(7179960520597631991)
XLA Ops:
  0.6 49.4 %shard_map.50 = (f32[128,256]{1,0:T(8,128)S(1)}, f32[128,256]{1,0:T(8,128)S(1)}) custom-call(bf16[128,256]{1,0:T(8,128)(2,1)} %q_hbm.1, bf16[128,256]{1,0:T(8,128)(2,1)} %p_hbm.1, s32[128,128]{1,0:T(8,128)} %bitcast.1), custom_call_target="tpu_custom_call" | custom-call | tf_op jit(solution)/shard_map/pallas_call | solution.py:409
  50.1 0.7 %copy.7 = f32[128,256]{1,0:T(8,128)} copy(f32[128,256]{1,0:T(8,128)S(1)} %get-tuple-element.2) | data formatting | bytes 262144
  50.7 0.7 %copy.8 = f32[128,256]{1,0:T(8,128)} copy(f32[128,256]{1,0:T(8,128)S(1)} %get-tuple-element.3) | data formatting | bytes 262144
